TPU v7x, 32 devices: a whole 2x2x4 slice. The times are simulated.
32 devices in a mesh: lat: 4 (over y, x), lon: 8 (over z, core).
Axes of the slice: x: 2, y: 2, z: 4, core: 2. Of those that a mesh axis runs over, the one named last changes fastest.
Arguments:
- input_field: bfloat16 [512, 512, 128], P('lat', 'lon'), may hold values from -6 to 6
- conv_one: bfloat16 [3, 3, 128, 128], replicated, may hold values from -0.1875 to 0.1875
- conv_two: bfloat16 [3, 3, 128, 128], replicated, may hold values from -0.1875 to 0.1875
- merge_weight: bfloat16 [512, 512], replicated, may hold values from -0.25 to 0.25
- norm_gains: float32 [4, 512], replicated, may hold values from 0.1 to 1.9
- attention_in: bfloat16 [512, 1536], replicated, may hold values from -0.25 to 0.25
- attention_out: bfloat16 [512, 512], replicated, may hold values from -0.25 to 0.25
- dense_in: bfloat16 [512, 2048], replicated, may hold values from -0.25 to 0.25
- dense_out: bfloat16 [2048, 512], replicated, may hold values from -0.125 to 0.125
- expand_weight: bfloat16 [512, 512], replicated, may hold values from -0.25 to 0.25
Outputs:
- output_field: bfloat16 [512, 512, 128], P('lat', 'lon')
All inputs are finite; a program needn't handle non-finite values.
Results may differ from a plain program's by a relative error of at most 0.0095.
Values may be sent and summed in bfloat16 or wider, within the bound.
A program may use at most 128 MiB of HBM per device.

v0:
```python
import functools
import math

import jax
import jax.numpy as jnp
from jax import lax
from jax.experimental import pallas as pl
from jax.experimental.pallas import tpu as pltpu
from jax.sharding import PartitionSpec as P

WINDOW = 16
HEAD_WIDTH = 32
EPSILON = 1e-06
FLOOR = 0.75
CHUNKS = 2
F32 = jnp.float32
BF16 = jnp.bfloat16
LIMIT = 56 * 1024 * 1024


def dot(a, b):
    return jnp.dot(a, b, preferred_element_type=F32)


def padded(cells, sides, width):
    for axis, dim in sides:
        count = lax.axis_size(axis)
        ends = count - 1
        head = lax.slice_in_dim(cells, 0, width, axis=dim)
        tail = lax.slice_in_dim(cells, cells.shape[dim] - width, cells.shape[dim], axis=dim)
        cells = jnp.concatenate(
            [
                lax.ppermute(tail, axis, [(i, (i + 1) % count) for i in range(ends)]),
                cells,
                lax.ppermute(head, axis, [((i + 1) % count, i) for i in range(ends)]),
            ],
            axis=dim,
        )
    return cells


def pair_kernel(kernel_ref, paired):
    taps, _, c, o = kernel_ref.shape
    zero = jnp.zeros((c, o), BF16)
    for a in range(taps):
        for b in range(4):
            rows = slice((4 * a + b) * c, (4 * a + b + 1) * c)
            paired[rows, :o] = kernel_ref[a, b] if b < 3 else zero
            paired[rows, o:] = kernel_ref[a, b - 1] if b > 0 else zero


def encode_body(geo, place_ref, x_ref, k1_ref, k2_ref, mw_ref, out_ref, xs, fs, cs, w1_ref, w2_ref):
    (chunk, chunks, per_lat, per_lon, offset_lat, offset_lon, lat_total, lon_total, breadth, pairs) = geo
    band = pl.program_id(0)
    rows = 2 * offset_lat // chunks
    c = x_ref.shape[2]
    half = breadth // 2
    wide = breadth + 4

    @pl.when(band == 0)
    def _():
        pair_kernel(k1_ref, w1_ref)
        pair_kernel(k2_ref, w2_ref)
        xs[:, wide:, :] = jnp.zeros((rows + 4, xs.shape[1] - wide, c), F32)

    xs[:, :wide, :] = x_ref[...].astype(F32)
    quad = [
        xs[:, pl.ds(j, pairs, stride=2), :].astype(BF16) for j in range(4)
    ]
    lhs = jnp.concatenate(
        [q[a : a + rows + 2].reshape((rows + 2) * pairs, c) for a in range(3) for q in quad], axis=1
    )
    first = jax.nn.gelu(dot(lhs, w1_ref[...])).reshape(rows + 2, pairs, 2 * c)
    row = lax.broadcasted_iota(jnp.int32, first.shape, 0)
    pair = lax.broadcasted_iota(jnp.int32, first.shape, 1)
    lane = lax.broadcasted_iota(jnp.int32, first.shape, 2)
    lat_place = row + (place_ref[0] + band * 2 * offset_lat + chunk * rows - 1)
    lon_place = 2 * pair + (lane >= c).astype(jnp.int32) + (place_ref[1] - 1)
    inside = (lat_place >= 0) & (lat_place < lat_total) & (lon_place >= 0) & (lon_place < lon_total)
    fs[...] = jnp.where(inside, first, 0.0)
    near = fs[:, 0:half, :].astype(BF16)
    far = fs[:, pl.ds(1, half), :].astype(BF16)
    lhs = jnp.concatenate(
        [q[a : a + rows].reshape(rows * half, 2 * c) for a in range(3) for q in (near, far)], axis=1
    )
    second = jax.nn.gelu(dot(lhs, w2_ref[...])).astype(BF16)
    second = second.reshape(rows // 2, 2, half, 2 * c)
    patches = jnp.concatenate(
        [second[:, d].reshape(rows // 2 * half, 2 * c) for d in range(2)], axis=1
    )
    coarse = dot(patches, mw_ref[...]).astype(BF16).reshape(rows // 2, half, 4 * c)
    for u in range(rows // 2):
        cs[u, pl.ds(pl.multiple_of(band * half, half), half), :] = coarse[u]

    @pl.when(band == per_lat - 1)
    def _():
        count = per_lat * half
        tokens = per_lat * per_lon
        to = lax.broadcasted_iota(jnp.int32, (count, count), 0)
        of = lax.broadcasted_iota(jnp.int32, (count, count), 1)
        source = (to % tokens) * offset_lon + to // tokens
        move = (of == source).astype(F32).astype(BF16)
        for u in range(rows // 2):
            out_ref[u * count : (u + 1) * count, :] = dot(move, cs[u]).astype(BF16)


def encode(geo, place, widened, w1, w2, merge_weight):
    (chunk, chunks, per_lat, per_lon, offset_lat, offset_lon, lat_total, lon_total, breadth, pairs) = geo
    rows = 2 * offset_lat // chunks
    c = widened.shape[2]
    half = breadth // 2
    count = rows // 2 * per_lat * half
    full = lambda a: pl.BlockSpec(a.shape, lambda p: (0,) * a.ndim)
    flops = 2 * per_lat * ((rows + 2) * pairs + rows * half) * 12 * c * 2 * c
    return pl.pallas_call(
        functools.partial(encode_body, geo),
        grid=(per_lat,),
        in_specs=[
            pl.BlockSpec(memory_space=pltpu.SMEM),
            pl.BlockSpec(
                (pl.Element(rows + 4), pl.Element(breadth + 4), pl.Element(c)),
                lambda p: (p * 2 * offset_lat + chunk * rows, 0, 0),
            ),
            full(w1),
            full(w2),
            full(merge_weight),
        ],
        out_specs=pl.BlockSpec((count, 4 * c), lambda p: (0, 0)),
        out_shape=jax.ShapeDtypeStruct((count, 4 * c), BF16),
        scratch_shapes=[
            pltpu.VMEM((rows + 4, max(2 * pairs + 8, breadth + 8), c), F32),
            pltpu.VMEM((rows + 2, pairs, 2 * c), F32),
            pltpu.VMEM((rows // 2, per_lat * half, 4 * c), BF16),
            pltpu.VMEM((12 * c, 2 * c), BF16),
            pltpu.VMEM((12 * c, 2 * c), BF16),
        ],
        compiler_params=pltpu.CompilerParams(
            dimension_semantics=("arbitrary",), vmem_limit_bytes=LIMIT
        ),
        cost_estimate=pl.CostEstimate(flops=flops, bytes_accessed=4_000_000, transcendentals=0),
        name="encode",
    )(place, widened, w1, w2, merge_weight)


def layer_norm(stream, gain):
    center = stream - jnp.mean(stream, axis=-1, keepdims=True)
    spread = jnp.mean(center * center, axis=-1, keepdims=True)
    return center * lax.rsqrt(spread + EPSILON) * gain


def window_body(geo, x_ref, g_ref, ai_ref, ao_ref, di_ref, do_ref, out_ref):
    devices, windows, tokens = geo
    latent = x_ref.shape[-1]
    size = devices * tokens
    count = windows * size
    to = lax.broadcasted_iota(jnp.int32, (count, count), 0)
    of = lax.broadcasted_iota(jnp.int32, (count, count), 1)
    row = lax.broadcasted_iota(jnp.int32, (count, 1), 0)
    col = lax.broadcasted_iota(jnp.int32, (1, count), 1)

    def sorted_row(i):
        return (i // tokens % windows) * size + i // (tokens * windows) * tokens + i % tokens

    gather = (to == sorted_row(col)).astype(F32).astype(BF16)
    scatter = (of == sorted_row(row)).astype(F32).astype(BF16)
    coarse = dot(gather, x_ref[...].reshape(count, latent))
    gains = g_ref[...]
    normed = layer_norm(coarse, gains[0:1]).astype(BF16)
    head_row = lax.broadcasted_iota(jnp.int32, (latent, latent), 0) // HEAD_WIDTH
    head_col = lax.broadcasted_iota(jnp.int32, (latent, latent), 1) // HEAD_WIDTH
    spread = jnp.where(head_row == head_col, 1.0 / HEAD_WIDTH, 0.0).astype(BF16)

    def head_norm(stream, gain):
        square = dot((stream * stream).astype(BF16), spread)
        return (stream * gain * lax.rsqrt(jnp.maximum(square, FLOOR))).astype(BF16)

    queries = head_norm(dot(normed, ai_ref[:, :latent]), gains[1:2])
    key_rows = head_norm(dot(normed, ai_ref[:, latent : 2 * latent]), gains[2:3])
    values = dot(normed, ai_ref[:, 2 * latent :]).astype(BF16)
    group = 128
    heads = group // HEAD_WIDTH
    lane = lax.broadcasted_iota(jnp.int32, (size, group), 1) // HEAD_WIDTH
    marks = [(lane == h).astype(F32).astype(BF16) for h in range(heads)]
    scale = HEAD_WIDTH ** (-0.5) * math.log2(math.e)
    parts = []
    for win in range(windows):
        span = slice(win * size, (win + 1) * size)
        row_parts = []
        for at in range(0, latent, group):
            q = queries[span, at : at + group]
            k = key_rows[span, at : at + group]
            v = values[span, at : at + group]
            expons = []
            stacked = []
            for h in range(heads):
                scores = lax.dot_general(
                    q * marks[h], k, (((1,), (1,)), ((), ())), preferred_element_type=F32
                )
                expons.append(jnp.exp2(scores * scale).astype(BF16))
                stacked.append(jnp.concatenate([v * marks[h], marks[h]], axis=1))
            both = dot(jnp.concatenate(expons, axis=1), jnp.concatenate(stacked, axis=0))
            row_parts.append((both[:, :group] / both[:, group:]).astype(BF16))
        parts.append(jnp.concatenate(row_parts, axis=1))
    attended = jnp.concatenate(parts, axis=0)
    mixed = (coarse + dot(attended, ao_ref[...])).astype(BF16)
    normed_two = layer_norm(mixed.astype(F32), gains[3:4]).astype(BF16)
    total = mixed.astype(F32)
    width = di_ref.shape[1]
    step = min(512, width)
    for at in range(0, width, step):
        inner = jax.nn.gelu(dot(normed_two, di_ref[:, at : at + step])).astype(BF16)
        total = total + dot(inner, do_ref[at : at + step, :])
    out_ref[...] = dot(scatter, total.astype(BF16)).astype(BF16).reshape(out_ref.shape)


def windows_of(geo, cells, gains, attention_in, attention_out, dense_in, dense_out):
    devices, windows, tokens = geo
    count, latent = cells.shape
    fits = [n for n in range(1, windows) if windows % n == 0 and n * tokens % 16 == 0]
    full = lambda a: pl.BlockSpec(a.shape, lambda i: (0,) * a.ndim)
    if fits:
        block = fits[0]
        cells = cells.reshape(devices, windows * tokens, latent)
        place = pl.BlockSpec((devices, block * tokens, latent), lambda i: (0, i, 0))
    else:
        block = windows
        place = full(cells)
    weights = (gains, attention_in, attention_out, dense_in, dense_out)
    flops = 2 * count * latent * (4 * latent + 2 * dense_in.shape[1] + 4 * count)
    made = pl.pallas_call(
        functools.partial(window_body, (devices, block, tokens)),
        grid=(windows // block,),
        out_shape=jax.ShapeDtypeStruct(cells.shape, BF16),
        in_specs=[place] + [full(a) for a in weights],
        out_specs=place,
        compiler_params=pltpu.CompilerParams(
            dimension_semantics=("arbitrary",), vmem_limit_bytes=LIMIT
        ),
        cost_estimate=pl.CostEstimate(flops=flops, bytes_accessed=8_000_000, transcendentals=0),
        name="windows",
    )(cells, *weights)
    return made.reshape(count, latent)


def expand_body(geo, aliased, ret_ref, x_ref, ew_ref, *rest):
    (chunk, chunks, per_lat, per_lon, offset_lat, offset_lon, breadth) = geo
    out_ref, os = rest[-2:]
    band = pl.program_id(0)
    lines = offset_lat // chunks
    c = x_ref.shape[2]
    half = breadth // 2
    tokens = per_lat * per_lon
    count = per_lat * half
    to = lax.broadcasted_iota(jnp.int32, (half, count), 0)
    of = lax.broadcasted_iota(jnp.int32, (half, count), 1)
    source = (to % offset_lon) * tokens + band * per_lon + to // offset_lon
    move = (of == source).astype(F32).astype(BF16)
    cells = jnp.concatenate(
        [dot(move, ret_ref[u * count : (u + 1) * count, :]).astype(BF16) for u in range(lines)], axis=0
    )
    made = dot(cells, ew_ref[...])
    for u in range(lines):
        for d in range(4):
            os[2 * u + d // 2, pl.ds(d % 2, half, stride=2), :] = made[
                u * half : (u + 1) * half, d * c : (d + 1) * c
            ]
    out_ref[...] = (os[...] + x_ref[...].astype(F32)).astype(BF16)


def expand(geo, returned, field, expand_weight, buffer):
    (chunk, chunks, per_lat, per_lon, offset_lat, offset_lon, breadth) = geo
    rows = 2 * offset_lat // chunks
    c = field.shape[2]
    aliased = buffer is not None
    place = pl.BlockSpec((rows, breadth, c), lambda p: (p * chunks + chunk, 0, 0))
    in_specs = [
        pl.BlockSpec(returned.shape, lambda p: (0, 0)),
        place,
        pl.BlockSpec(expand_weight.shape, lambda p: (0, 0)),
    ]
    args = [returned, field, expand_weight]
    if aliased:
        in_specs.append(pl.BlockSpec(memory_space=pl.ANY))
        args.append(buffer)
    return pl.pallas_call(
        functools.partial(expand_body, geo, aliased),
        grid=(per_lat,),
        in_specs=in_specs,
        out_specs=place,
        out_shape=jax.ShapeDtypeStruct(field.shape, BF16),
        scratch_shapes=[pltpu.VMEM((rows, breadth, c), F32)],
        input_output_aliases={3: 0} if aliased else {},
        compiler_params=pltpu.CompilerParams(
            dimension_semantics=("arbitrary",), vmem_limit_bytes=LIMIT
        ),
        cost_estimate=pl.CostEstimate(
            flops=2 * returned.size * 4 * c, bytes_accessed=3_000_000, transcendentals=0
        ),
        name="expand",
    )(*args)


def per_device(
    input_field,
    conv_one,
    conv_two,
    merge_weight,
    norm_gains,
    attention_in,
    attention_out,
    dense_in,
    dense_out,
    expand_weight,
):
    height, breadth, _ = input_field.shape
    latent = merge_weight.shape[1]
    lat_count = lax.axis_size("lat")
    lon_count = lax.axis_size("lon")
    per_lat = WINDOW // lat_count
    per_lon = WINDOW // lon_count
    offset_lat = height // (2 * per_lat)
    offset_lon = breadth // (2 * per_lon)
    tokens = per_lat * per_lon
    devices = lat_count * lon_count
    windows = offset_lat * offset_lon // devices // CHUNKS
    pairs = -(-(breadth // 2 + 1) // 16) * 16
    place = jnp.stack([lax.axis_index("lat") * height, lax.axis_index("lon") * breadth]).astype(jnp.int32)
    widened = padded(input_field, (("lat", 0), ("lon", 1)), 2)

    def exchange(cells):
        moved = lax.all_to_all(
            cells.reshape(devices, windows * tokens, latent),
            ("lat", "lon"),
            split_axis=0,
            concat_axis=0,
            tiled=True,
        )
        return moved.reshape(cells.shape)

    shape = (per_lat, per_lon, offset_lat, offset_lon)
    sent = [
        exchange(
            encode(
                (chunk, CHUNKS) + shape + (height * lat_count, breadth * lon_count, breadth, pairs),
                place,
                widened,
                conv_one,
                conv_two,
                merge_weight,
            )
        )
        for chunk in range(CHUNKS)
    ]
    returned = [
        exchange(
            windows_of(
                (devices, windows, tokens), cells, norm_gains, attention_in, attention_out, dense_in, dense_out
            )
        )
        for cells in sent
    ]
    out = None
    for chunk, cells in enumerate(returned):
        out = expand((chunk, CHUNKS) + shape + (breadth,), cells, input_field, expand_weight, out)
    return out


def solution(mesh):
    return jax.shard_map(
        per_device,
        mesh=mesh,
        in_specs=(P("lat", "lon", None), P(), P(), P(), P(), P(), P(), P(), P(), P()),
        out_specs=P("lat", "lon", None),
        check_vma=False,
    )
```

profile of v0, /device:TPU:0, one launch (start us, length us, event | category | flops | bytes accessed | tf_op | source)
XLA Modules:
  0.0 165.5 jit_solution(3244280781358291343)
XLA Ops:
  0.0 0.8 fusion.1
  0.8 4.9 %collective-permute-start = (bf16[2,64,128]{2,1,0:T(8,128)(2,1)S(1)}, bf16[2,64,128]{2,1,0:T(8,128)(2,1)S(1)}, u32[]{:S(2)}, u32[]{:S(2)}) collective-permute-start(bf16[2,64,128]{2,1,0:T(8,128)(2,1)S(1)} %get-tuple-element.8), channel_id=1, source_target_pairs={{0,8},{8,16},{16,24},{1,9},{9,17},{17,25},{2,10},{10,18},{18,26},{... | collective-permute-start | bytes 98312 | tf_op jit(solution)/shard_map/ppermute | solution.py:33
  5.6 1.3 collective-permute-start.1
  7.0 0.3 collective-permute-done
  7.2 1.9 %constant_dynamic-update-slice_fusion.1 = bf16[132,64,128]{2,1,0:T(8,128)(2,1)S(1)} fusion(bf16[132,64,128]{2,1,0:T(8,128)(2,1)S(1)} %constant_dynamic-update-slice_fusion.2, bf16[128,64,128]{2,1,0:T(8,128)(2,1)} %x_ref.3), kind=kLoop, calls=%fused_computation.2 | loop fusion | bytes 4194304
  9.1 2.3 %collective-permute-done.1 = bf16[2,64,128]{2,1,0:T(8,128)(2,1)S(1)} collective-permute-done((bf16[2,64,128]{2,1,0:T(8,128)(2,1)S(1)}, bf16[2,64,128]{2,1,0:T(8,128)(2,1)S(1)}, u32[]{:S(2)}, u32[]{:S(2)}) %collective-permute-start.1) | collective-permute-done | bytes 32800 | tf_op jit(solution)/shard_map/ppermute | solution.py:35
  11.5 0.1 fusion
  11.6 1.3 collective-permute-start.2
  12.9 1.3 collective-permute-start.3
  14.2 0.6 pad_add_fusion.place_ref
  14.8 0.0 collective-permute-done.2
  14.8 3.1 %collective-permute-done.3 = bf16[132,2,128]{2,1,0:T(2,128)(2,1)S(1)} collective-permute-done((bf16[132,2,128]{2,1,0:T(2,128)(2,1)S(1)}, bf16[132,2,128]{2,1,0:T(2,128)(2,1)S(1)}, u32[]{:S(2)}, u32[]{:S(2)}) %collective-permute-start.3) | collective-permute-done | bytes 67616 | tf_op jit(solution)/shard_map/ppermute | solution.py:35
  17.8 2.9 %pad_maximum_fusion.x_ref = bf16[132,68,128]{2,1,0:T(8,128)(2,1)} fusion(bf16[132,2,128]{2,1,0:T(2,128)(2,1)S(1)} %collective-permute-done.3, bf16[132,64,128]{2,1,0:T(8,128)(2,1)S(1)} %constant_dynamic-update-slice_fusion, bf16[132,2,128]{2,1,0:T(2,128)(2,1)S(1)} %collective-permute-done.2), kind=kLoop, calls=%fused_computation | loop fusion | flops 6893568 | bytes 4595712 | tf_op jit(solution)/shard_map/concatenate | solution.py:31
  20.7 13.8 %encode.3 = bf16[1024,512]{1,0:T(8,128)(2,1)} custom-call(s32[2]{0:T(128)} %pad_add_fusion.place_ref, bf16[132,68,128]{2,1,0:T(8,128)(2,1)} %pad_maximum_fusion.x_ref, bf16[3,3,128,128]{3,2,1,0:T(8,128)(2,1)} %k1_ref.3, bf16[3,3,128,128]{3,2,1,0:T(8,128)(2,1)} %k2_ref.3, bf16[512,512]{1,0:T(8,128)(2,1)} %mw_ref.3), custom_call_target="tpu_custom_call" | custom-call | flops 4328521728 | bytes 4000000 | tf_op jit(solution)/shard_map/encode/pallas_call | solution.py:115
  34.5 7.3 %all-to-all-start.2 = ((bf16[32,32,512]{2,1,0:T(8,128)(2,1)}), bf16[32,32,512]{2,1,0:T(8,128)(2,1)S(1)}, u32[]{:S(2)}, u32[]{:S(2)}) async-start(bf16[32,32,512]{2,1,0:T(8,128)(2,1)} %bitcast.9), calls=%async_computation.2 | async-start | bytes 2097152 | tf_op jit(solution)/shard_map/all_to_all | solution.py:331
  41.8 13.8 %encode.2 = bf16[1024,512]{1,0:T(8,128)(2,1)} custom-call(s32[2]{0:T(128)} %pad_add_fusion.place_ref, bf16[132,68,128]{2,1,0:T(8,128)(2,1)} %pad_maximum_fusion.x_ref, bf16[3,3,128,128]{3,2,1,0:T(8,128)(2,1)} %k1_ref.3, bf16[3,3,128,128]{3,2,1,0:T(8,128)(2,1)} %k2_ref.3, bf16[512,512]{1,0:T(8,128)(2,1)} %mw_ref.3), custom_call_target="tpu_custom_call" | custom-call | flops 4328521728 | bytes 4000000 | tf_op jit(solution)/shard_map/encode/pallas_call | solution.py:115
  55.6 13.7 %all-to-all-done.2.x_ref = bf16[32,32,512]{2,1,0:T(8,128)(2,1)S(1)} async-done(((bf16[32,32,512]{2,1,0:T(8,128)(2,1)}), bf16[32,32,512]{2,1,0:T(8,128)(2,1)S(1)}, u32[]{:S(2)}, u32[]{:S(2)}) %all-to-all-start.2) | async-done | bytes 1048608 | tf_op jit(solution)/shard_map/all_to_all | solution.py:331
  69.3 0.0 copy-start.2
  69.3 2.8 %all-to-all-start = ((bf16[32,32,512]{2,1,0:T(8,128)(2,1)}), bf16[32,32,512]{2,1,0:T(8,128)(2,1)S(1)}, u32[]{:S(2)}, u32[]{:S(2)}) async-start(bf16[32,32,512]{2,1,0:T(8,128)(2,1)} %bitcast.8), calls=%async_computation | async-start | bytes 2097152 | tf_op jit(solution)/shard_map/all_to_all | solution.py:331
  72.1 0.0 copy-done.2
  72.2 20.4 %windows.3 = bf16[32,32,512]{2,1,0:T(8,128)(2,1)} custom-call(bf16[32,32,512]{2,1,0:T(8,128)(2,1)} %copy-done.2, f32[4,512]{1,0:T(4,128)} %g_ref.3, bf16[512,1536]{1,0:T(8,128)(2,1)} %ai_ref.3, bf16[512,512]{1,0:T(8,128)(2,1)} %ao_ref.3, bf16[512,2048]{1,0:T(8,128)(2,1)} %di_ref.3, bf16[2048,512]{1,0:T(8,128)(2,1)} %do_ref.3), custom_call_target="tpu_custom_call" | custom-call | flops 10737418240 | bytes 8000000 | tf_op jit(solution)/shard_map/windows/pallas_call | solution.py:230
  92.5 6.9 %all-to-all-done.x_ref = bf16[32,32,512]{2,1,0:T(8,128)(2,1)S(1)} async-done(((bf16[32,32,512]{2,1,0:T(8,128)(2,1)}), bf16[32,32,512]{2,1,0:T(8,128)(2,1)S(1)}, u32[]{:S(2)}, u32[]{:S(2)}) %all-to-all-start) | async-done | bytes 1048608 | tf_op jit(solution)/shard_map/all_to_all | solution.py:331
  99.4 2.9 %all-to-all-start.3 = ((bf16[32,32,512]{2,1,0:T(8,128)(2,1)}), bf16[32,32,512]{2,1,0:T(8,128)(2,1)S(1)}, u32[]{:S(2)}, u32[]{:S(2)}) async-start(bf16[32,32,512]{2,1,0:T(8,128)(2,1)} %windows.3), calls=%async_computation.3 | async-start | bytes 2097152 | tf_op jit(solution)/shard_map/all_to_all | solution.py:331
  102.3 0.0 copy-done.3
  102.3 20.4 %windows.2 = bf16[32,32,512]{2,1,0:T(8,128)(2,1)} custom-call(bf16[32,32,512]{2,1,0:T(8,128)(2,1)} %copy-done.3, f32[4,512]{1,0:T(4,128)} %g_ref.3, bf16[512,1536]{1,0:T(8,128)(2,1)} %ai_ref.3, bf16[512,512]{1,0:T(8,128)(2,1)} %ao_ref.3, bf16[512,2048]{1,0:T(8,128)(2,1)} %di_ref.3, bf16[2048,512]{1,0:T(8,128)(2,1)} %do_ref.3), custom_call_target="tpu_custom_call" | custom-call | flops 10737418240 | bytes 8000000 | tf_op jit(solution)/shard_map/windows/pallas_call | solution.py:230
  122.7 6.9 %all-to-all-done.3 = bf16[32,32,512]{2,1,0:T(8,128)(2,1)S(1)} async-done(((bf16[32,32,512]{2,1,0:T(8,128)(2,1)}), bf16[32,32,512]{2,1,0:T(8,128)(2,1)S(1)}, u32[]{:S(2)}, u32[]{:S(2)}) %all-to-all-start.3) | async-done | bytes 1048608 | tf_op jit(solution)/shard_map/all_to_all | solution.py:331
  129.6 2.6 %all-to-all-start.1 = ((bf16[32,32,512]{2,1,0:T(8,128)(2,1)}), bf16[32,32,512]{2,1,0:T(8,128)(2,1)S(1)}, u32[]{:S(2)}, u32[]{:S(2)}) async-start(bf16[32,32,512]{2,1,0:T(8,128)(2,1)} %windows.2), calls=%async_computation.1 | async-start | bytes 2097152 | tf_op jit(solution)/shard_map/all_to_all | solution.py:331
  132.2 0.0 copy-done.1
  132.2 4.8 %expand.2.rest_0_ = bf16[128,64,128]{2,1,0:T(8,128)(2,1)} custom-call(bf16[1024,512]{1,0:T(8,128)(2,1)} %bitcast.7, bf16[128,64,128]{2,1,0:T(8,128)(2,1)} %x_ref.3, bf16[512,512]{1,0:T(8,128)(2,1)} %ew_ref.3), custom_call_target="tpu_custom_call" | custom-call | flops 536870912 | bytes 3000000 | tf_op jit(solution)/shard_map/expand/pallas_call | solution.py:285
  137.0 22.6 %all-to-all-done.1 = bf16[32,32,512]{2,1,0:T(8,128)(2,1)S(1)} async-done(((bf16[32,32,512]{2,1,0:T(8,128)(2,1)}), bf16[32,32,512]{2,1,0:T(8,128)(2,1)S(1)}, u32[]{:S(2)}, u32[]{:S(2)}) %all-to-all-start.1) | async-done | bytes 1048608 | tf_op jit(solution)/shard_map/all_to_all | solution.py:331
  159.7 1.0 copy-done
  160.7 4.8 %expand.3 = bf16[128,64,128]{2,1,0:T(8,128)(2,1)} custom-call(bf16[1024,512]{1,0:T(8,128)(2,1)} %bitcast.6, bf16[128,64,128]{2,1,0:T(8,128)(2,1)} %x_ref.3, bf16[512,512]{1,0:T(8,128)(2,1)} %ew_ref.3, bf16[128,64,128]{2,1,0:T(8,128)(2,1)} %expand.2.rest_0_), custom_call_target="tpu_custom_call", output_to_operand_aliasing={{}: (3, {})} | custom-call | flops 536870912 | bytes 3000000 | tf_op jit(solution)/shard_map/expand/pallas_call | solution.py:285
  (5 shorter events, 0.0 us)
Async XLA Ops:
  0.8 6.4 %collective-permute-start = (bf16[2,64,128]{2,1,0:T(8,128)(2,1)S(1)}, bf16[2,64,128]{2,1,0:T(8,128)(2,1)S(1)}, u32[]{:S(2)}, u32[]{:S(2)}) collective-permute-start(bf16[2,64,128]{2,1,0:T(8,128)(2,1)S(1)} %get-tuple-element.8), channel_id=1, source_target_pairs={{0,8},{8,16},{16,24},{1,9},{9,17},{17,25},{2,10},{10,18},{18,26},{... | collective-permute-start | bytes 98312 | tf_op jit(solution)/shard_map/ppermute | solution.py:33
  5.6 5.8 %collective-permute-start.1 = (bf16[2,64,128]{2,1,0:T(8,128)(2,1)S(1)}, bf16[2,64,128]{2,1,0:T(8,128)(2,1)S(1)}, u32[]{:S(2)}, u32[]{:S(2)}) collective-permute-start(bf16[2,64,128]{2,1,0:T(8,128)(2,1)S(1)} %get-tuple-element.7), channel_id=1, source_target_pairs={{8,0},{16,8},{24,16},{9,1},{17,9},{25,17},{10,2},{18,10},{26,18},{... | collective-permute-start | bytes 98312 | tf_op jit(solution)/shard_map/ppermute | solution.py:35
  11.6 3.2 %collective-permute-start.2 = (bf16[132,2,128]{2,1,0:T(2,128)(2,1)S(1)}, bf16[132,2,128]{2,1,0:T(2,128)(2,1)S(1)}, u32[]{:S(2)}, u32[]{:S(2)}) collective-permute-start(bf16[132,2,128]{2,1,0:T(2,128)(2,1)S(1)} %get-tuple-element.5), channel_id=1, source_target_pairs={{0,1},{1,2},{2,3},{3,4},{4,5},{5,6},{6,7},{8,9},{9,10},{10,11},{11... | collective-permute-start | bytes 202760 | tf_op jit(solution)/shard_map/ppermute | solution.py:33
  12.9 5.0 %collective-permute-start.3 = (bf16[132,2,128]{2,1,0:T(2,128)(2,1)S(1)}, bf16[132,2,128]{2,1,0:T(2,128)(2,1)S(1)}, u32[]{:S(2)}, u32[]{:S(2)}) collective-permute-start(bf16[132,2,128]{2,1,0:T(2,128)(2,1)S(1)} %get-tuple-element.6), channel_id=1, source_target_pairs={{1,0},{2,1},{3,2},{4,3},{5,4},{6,5},{7,6},{9,8},{10,9},{11,10},{12... | collective-permute-start | bytes 202760 | tf_op jit(solution)/shard_map/ppermute | solution.py:35
  34.5 34.8 %all-to-all-start.2 = ((bf16[32,32,512]{2,1,0:T(8,128)(2,1)}), bf16[32,32,512]{2,1,0:T(8,128)(2,1)S(1)}, u32[]{:S(2)}, u32[]{:S(2)}) async-start(bf16[32,32,512]{2,1,0:T(8,128)(2,1)} %bitcast.9), calls=%async_computation.2 | async-start | bytes 2097152 | tf_op jit(solution)/shard_map/all_to_all | solution.py:331
  69.3 2.8 %copy-start.2 = (bf16[32,32,512]{2,1,0:T(8,128)(2,1)}, bf16[32,32,512]{2,1,0:T(8,128)(2,1)S(1)}, u32[]{:S(2)}) copy-start(bf16[32,32,512]{2,1,0:T(8,128)(2,1)S(1)} %all-to-all-done.2.x_ref) | copy-start | bytes 3145732
  69.3 30.1 %all-to-all-start = ((bf16[32,32,512]{2,1,0:T(8,128)(2,1)}), bf16[32,32,512]{2,1,0:T(8,128)(2,1)S(1)}, u32[]{:S(2)}, u32[]{:S(2)}) async-start(bf16[32,32,512]{2,1,0:T(8,128)(2,1)} %bitcast.8), calls=%async_computation | async-start | bytes 2097152 | tf_op jit(solution)/shard_map/all_to_all | solution.py:331
  99.4 2.9 %copy-start.3 = (bf16[32,32,512]{2,1,0:T(8,128)(2,1)}, bf16[32,32,512]{2,1,0:T(8,128)(2,1)S(1)}, u32[]{:S(2)}) copy-start(bf16[32,32,512]{2,1,0:T(8,128)(2,1)S(1)} %all-to-all-done.x_ref) | copy-start | bytes 3145732
  99.4 30.1 %all-to-all-start.3 = ((bf16[32,32,512]{2,1,0:T(8,128)(2,1)}), bf16[32,32,512]{2,1,0:T(8,128)(2,1)S(1)}, u32[]{:S(2)}, u32[]{:S(2)}) async-start(bf16[32,32,512]{2,1,0:T(8,128)(2,1)} %windows.3), calls=%async_computation.3 | async-start | bytes 2097152 | tf_op jit(solution)/shard_map/all_to_all | solution.py:331
  129.6 2.7 %copy-start.1 = (bf16[32,32,512]{2,1,0:T(8,128)(2,1)}, bf16[32,32,512]{2,1,0:T(8,128)(2,1)S(1)}, u32[]{:S(2)}) copy-start(bf16[32,32,512]{2,1,0:T(8,128)(2,1)S(1)} %all-to-all-done.3) | copy-start | bytes 3145732
  129.6 30.1 %all-to-all-start.1 = ((bf16[32,32,512]{2,1,0:T(8,128)(2,1)}), bf16[32,32,512]{2,1,0:T(8,128)(2,1)S(1)}, u32[]{:S(2)}, u32[]{:S(2)}) async-start(bf16[32,32,512]{2,1,0:T(8,128)(2,1)} %windows.2), calls=%async_computation.1 | async-start | bytes 2097152 | tf_op jit(solution)/shard_map/all_to_all | solution.py:331
  159.7 1.0 copy-start
where the time goes:
time: 166 us; the launch traced here: 165 us
  Pallas kernels  77.9 us (47%)
  waiting for transfers between devices  55.7 us (34%)
  starting transfers between devices  24.4 us (15%)
  local copies, waits for them, and re-layouts  3.79 us (2%)
  other arithmetic  3.47 us (2%)
    all_to_all x4, waiting for transfers between devices, exchange(): lax.all_to_all(cells.reshape(devices, windows * tokens, latent), ('lat',...  50.1 us
    pallas_call x2, Pallas kernels, windows_of(): pl.pallas_call(functools.partial(window_body, (devices, block, tokens)),...  40.8 us
    pallas_call x2, Pallas kernels, encode(): pl.pallas_call(functools.partial(encode_body, geo), grid=(per_lat,), in_s...  27.5 us
    all_to_all x4, starting transfers between devices, exchange(): lax.all_to_all(cells.reshape(devices, windows * tokens, latent), ('lat',...  15.7 us
    pallas_call x2, Pallas kernels, expand(): pl.pallas_call(functools.partial(expand_body, geo, aliased), grid=(per_la...  9.62 us
    ppermute x2, starting transfers between devices, padded(): lax.ppermute(tail, axis, [(i, (i + 1) % count) for i in range(ends)])  6.15 us
    ppermute x2, waiting for transfers between devices, padded(): lax.ppermute(head, axis, [((i + 1) % count, i) for i in range(ends)])  5.38 us
  transfers between devices with their start and end apart: 8, of which 7 were waited for; matrix products, arithmetic and copies ran while one was open for 2% of the time, Pallas kernels for 36%

commit v1 on v0

v1 whole, which is shorter than its diff:
```python
import functools
import math

import jax
import jax.numpy as jnp
from jax import lax
from jax.experimental import pallas as pl
from jax.experimental.pallas import tpu as pltpu
from jax.sharding import PartitionSpec as P

WINDOW = 16
HEAD_WIDTH = 32
EPSILON = 1e-06
FLOOR = 0.75
F32 = jnp.float32
BF16 = jnp.bfloat16
LIMIT = 60 * 1024 * 1024
MESH = pl.DeviceIdType.MESH
LEAD = 8
UNIT = 2


def dot(a, b):
    return jnp.dot(a, b, preferred_element_type=F32)


def ones_where(flag):
    return flag.astype(F32).astype(BF16)


def pair_kernel(kernel_ref, paired):
    taps, _, c, o = kernel_ref.shape
    zero = jnp.zeros((c, o), BF16)
    for a in range(taps):
        for b in range(4):
            rows = slice((4 * a + b) * c, (4 * a + b + 1) * c)
            paired[rows, :o] = kernel_ref[a, b] if b < 3 else zero
            paired[rows, o:] = kernel_ref[a, b - 1] if b > 0 else zero


def layer_norm(stream, gain):
    center = stream - jnp.mean(stream, axis=-1, keepdims=True)
    spread = jnp.mean(center * center, axis=-1, keepdims=True)
    return center * lax.rsqrt(spread + EPSILON) * gain


def window_block(windows, sources, tokens, cells, g_ref, ai_ref, ao_ref, di_ref, do_ref):
    latent = cells.shape[-1]
    size = sources * tokens
    count = windows * size
    coarse = cells
    if windows > 1:
        to = lax.broadcasted_iota(jnp.int32, (count, count), 0)
        of = lax.broadcasted_iota(jnp.int32, (count, count), 1)
        row = lax.broadcasted_iota(jnp.int32, (count, 1), 0)
        col = lax.broadcasted_iota(jnp.int32, (1, count), 1)

        def sorted_row(i):
            return (i // tokens % windows) * size + i // (tokens * windows) * tokens + i % tokens

        gather = ones_where(to == sorted_row(col))
        scatter = ones_where(of == sorted_row(row))
        coarse = dot(gather, cells.astype(BF16))
    gains = g_ref[...]
    normed = layer_norm(coarse, gains[0:1]).astype(BF16)
    head_row = lax.broadcasted_iota(jnp.int32, (latent, latent), 0) // HEAD_WIDTH
    head_col = lax.broadcasted_iota(jnp.int32, (latent, latent), 1) // HEAD_WIDTH
    spread = jnp.where(head_row == head_col, 1.0 / HEAD_WIDTH, 0.0).astype(BF16)

    def head_norm(stream, gain):
        square = dot((stream * stream).astype(BF16), spread)
        return (stream * gain * lax.rsqrt(jnp.maximum(square, FLOOR))).astype(BF16)

    queries = head_norm(dot(normed, ai_ref[:, :latent]), gains[1:2])
    key_rows = head_norm(dot(normed, ai_ref[:, latent : 2 * latent]), gains[2:3])
    values = dot(normed, ai_ref[:, 2 * latent :]).astype(BF16)
    group = 128
    heads = group // HEAD_WIDTH
    lane = lax.broadcasted_iota(jnp.int32, (size, group), 1) // HEAD_WIDTH
    marks = [ones_where(lane == h) for h in range(heads)]
    scale = HEAD_WIDTH ** (-0.5) * math.log2(math.e)
    parts = []
    for win in range(windows):
        span = slice(win * size, (win + 1) * size)
        row_parts = []
        for at in range(0, latent, group):
            q = queries[span, at : at + group]
            k = key_rows[span, at : at + group]
            v = values[span, at : at + group]
            expons = []
            stacked = []
            for h in range(heads):
                scores = lax.dot_general(
                    q * marks[h], k, (((1,), (1,)), ((), ())), preferred_element_type=F32
                )
                expons.append(jnp.exp2(scores * scale).astype(BF16))
                stacked.append(jnp.concatenate([v * marks[h], marks[h]], axis=1))
            both = dot(jnp.concatenate(expons, axis=1), jnp.concatenate(stacked, axis=0))
            row_parts.append((both[:, :group] / both[:, group:]).astype(BF16))
        parts.append(jnp.concatenate(row_parts, axis=1))
    attended = jnp.concatenate(parts, axis=0)
    mixed = (coarse + dot(attended, ao_ref[...])).astype(BF16)
    normed_two = layer_norm(mixed.astype(F32), gains[3:4]).astype(BF16)
    total = mixed.astype(F32)
    width = di_ref.shape[1]
    step = min(512, width)
    for at in range(0, width, step):
        inner = jax.nn.gelu(dot(normed_two, di_ref[:, at : at + step])).astype(BF16)
        total = total + dot(inner, do_ref[at : at + step, :])
    if windows > 1:
        total = dot(scatter, total.astype(BF16))
    return total


def whole_body(geo, x_hbm, k1_hbm, k2_hbm, mw_hbm, g_hbm, ai_hbm, ao_hbm, di_hbm, do_hbm, ew_hbm, out_hbm,
               xv, k1_ref, k2_ref, mw_ref, g_ref, ai_ref, ao_ref, di_ref, do_ref, ew_ref,
               w1_ref, w2_ref, xs, xn, xf, fs, fn, ff, edges, sides, caps, corners,
               sbuf, rbuf, s2buf, r2buf, os, ost,
               load_sem, halo_send, halo_recv, go_send, go_recv, back_send, back_recv, out_sem):
    (nlat, nlon, bands, per_lon, offset_lat, offset_lon, pairs, joint, groups) = geo
    count = nlat * nlon
    lat = lax.axis_index("lat")
    lon = lax.axis_index("lon")
    me = lat * nlon + lon
    height, breadth, c = xv.shape
    half = breadth // 2
    latent = 4 * c
    tokens = bands * per_lon
    cells = bands * half
    reach = 2 * offset_lat
    rows = 2 * UNIT
    steps = offset_lat // UNIT
    block = UNIT * offset_lon // joint
    pitch = xs.shape[0] // (height + 4)

    barrier = pltpu.get_barrier_semaphore()

    def greet(k, carry):
        peer = (me + k) % count
        pl.semaphore_signal(barrier, inc=1, device_id=(peer // nlon, peer % nlon), device_id_type=MESH)
        return carry

    lax.fori_loop(1, count, greet, 0)

    loads = [
        pltpu.make_async_copy(a, b, load_sem.at[i])
        for i, (a, b) in enumerate(
            [(x_hbm, xv), (k1_hbm, k1_ref), (k2_hbm, k2_ref), (mw_hbm, mw_ref), (g_hbm, g_ref),
             (ai_hbm, ai_ref), (ao_hbm, ao_ref), (di_hbm, di_ref), (do_hbm, do_ref), (ew_hbm, ew_ref)]
        )
    ]
    for load in loads:
        load.start()
    loads[0].wait()

    def widen(r, carry):
        for k in range(4):
            at = 4 * r + k
            xs[pl.ds((at + 2) * pitch + LEAD, breadth), :] = xv[at].astype(F32)
        return carry

    lax.fori_loop(0, height // 4, widen, 0)

    def column(at):
        return xs[pl.ds(2 * pitch + LEAD + at, height, stride=pitch), :]

    for side, at in enumerate((0, breadth - 2)):
        edges[side] = jnp.concatenate([column(at), column(at + 1)], axis=1).astype(BF16)

    pl.semaphore_wait(barrier, count - 1)

    tip = 16
    ends = (slice(0, tip), slice(height - tip, height))
    halo = []
    for i, (dy, dx) in enumerate(((-1, 0), (1, 0), (0, -1), (0, 1), (-1, -1), (-1, 1), (1, -1), (1, 1))):
        if dx == 0:
            src = xv.at[pl.ds(0 if dy < 0 else height - 2, 2)]
            dst = caps.at[1 if dy < 0 else 0]
        elif dy == 0:
            src = edges.at[0 if dx < 0 else 1]
            dst = sides.at[1 if dx < 0 else 0]
        else:
            first = 0 if dy < 0 else height - tip
            src = edges.at[0 if dx < 0 else 1, pl.ds(first, tip)]
            dst = corners.at[(2 if dy < 0 else 0) + (1 if dx < 0 else 0)]
        there = (lat + dy >= 0) & (lat + dy < nlat) & (lon + dx >= 0) & (lon + dx < nlon)
        back = (lat - dy >= 0) & (lat - dy < nlat) & (lon - dx >= 0) & (lon - dx < nlon)
        copy = pltpu.make_async_remote_copy(
            src_ref=src, dst_ref=dst, send_sem=halo_send.at[i], recv_sem=halo_recv.at[i],
            device_id=(jnp.clip(lat + dy, 0, nlat - 1), jnp.clip(lon + dx, 0, nlon - 1)), device_id_type=MESH,
        )
        halo.append((dy, dx, there, back, copy))
        pl.when(there)(copy.start)

    loads[1].wait()
    pair_kernel(k1_ref, w1_ref)
    loads[2].wait()
    pair_kernel(k2_ref, w2_ref)
    loads[3].wait()

    left, right = LEAD - 2, LEAD + breadth
    for dy, dx, there, back, copy in halo:
        row = 0 if dy > 0 else height + 2
        col = left if dx > 0 else right

        def landed(dy=dy, dx=dx, copy=copy, row=row, col=col):
            copy.wait_recv()
            if dx == 0:
                for k in range(2):
                    xs[pl.ds((row + k) * pitch + LEAD, breadth), :] = caps[0 if dy > 0 else 1, k].astype(F32)
            elif dy == 0:
                value = sides[0 if dx > 0 else 1].astype(F32)
                for k in range(2):
                    xs[pl.ds(2 * pitch + col + k, height, stride=pitch), :] = value[:, k * c : (k + 1) * c]
            else:
                value = corners[(0 if dy > 0 else 2) + (0 if dx > 0 else 1)].astype(F32)
                base = tip - 2 if dy > 0 else 0
                for r in range(2):
                    for k in range(2):
                        xs[pl.ds((row + r) * pitch + col + k, 1), :] = value[
                            base + r : base + r + 1, k * c : (k + 1) * c
                        ]

        def empty(dy=dy, dx=dx, row=row, col=col):
            if dx == 0:
                for k in range(2):
                    xs[pl.ds((row + k) * pitch + LEAD, breadth), :] = jnp.zeros((breadth, c), F32)
            elif dy == 0:
                for k in range(2):
                    xs[pl.ds(2 * pitch + col + k, height, stride=pitch), :] = jnp.zeros((height, c), F32)
            else:
                for r in range(2):
                    for k in range(2):
                        xs[pl.ds((row + r) * pitch + col + k, 1), :] = jnp.zeros((1, c), F32)

        pl.when(back)(landed)
        pl.when(jnp.logical_not(back))(empty)

    def fill(start, n):
        for r in range(n):
            base = (start + r) * pitch + left
            quad = [xs[pl.ds(base + j, pairs, stride=2), :] for j in range(4)]
            xn[pl.ds(start + r, 1)] = jnp.concatenate(quad[:2], axis=1).astype(BF16)[None]
            xf[pl.ds(start + r, 1)] = jnp.concatenate(quad[2:], axis=1).astype(BF16)[None]

    pair = lax.broadcasted_iota(jnp.int32, (pairs, 2 * c), 0)
    lane = lax.broadcasted_iota(jnp.int32, (pairs, 2 * c), 1)
    lon_place = 2 * pair + (lane >= c).astype(jnp.int32) + (lon * breadth - 1)
    inside = (lon_place >= 0) & (lon_place < nlon * breadth)

    def conv_one(starts, n):
        lhs = jnp.concatenate(
            [
                jnp.concatenate(
                    [buf[pl.ds(start + a, n)].reshape(n * pairs, 2 * c) for start in starts], axis=0
                )
                for a in range(3)
                for buf in (xn, xf)
            ],
            axis=1,
        )
        first = jax.nn.gelu(dot(lhs, w1_ref[...])).reshape(bands * n, pairs, 2 * c)
        fs[: bands * n] = jnp.where(inside[None], first, 0.0)
        for p, start in enumerate(starts):
            fn[pl.ds(start, n)] = fs[p * n : (p + 1) * n, 0:half, :].astype(BF16)
            ff[pl.ds(start, n)] = fs[p * n : (p + 1) * n, pl.ds(1, half), :].astype(BF16)

    nothing = jnp.zeros((1, half, 2 * c), BF16)
    for p in range(bands):
        fill(p * reach, 4)
    conv_one([p * reach for p in range(bands)], 2)

    @pl.when(lat == 0)
    def _():
        fn[0:1] = nothing
        ff[0:1] = nothing

    to = lax.broadcasted_iota(jnp.int32, (cells, cells), 0)
    of = lax.broadcasted_iota(jnp.int32, (cells, cells), 1)
    outward = ones_where(of == (to % tokens) * offset_lon + to // tokens)
    inward = ones_where(of == (to % offset_lon) * tokens + to // offset_lon)

    def forward(entry):
        peer = entry % count
        return pltpu.make_async_remote_copy(
            src_ref=sbuf.at[pl.ds(entry, 1)], dst_ref=rbuf.at[pl.ds(entry // count * count + me, 1)],
            send_sem=go_send.at[entry // count], recv_sem=go_recv.at[entry // count],
            device_id=(peer // nlon, peer % nlon), device_id_type=MESH,
        )

    def encode(e, carry):
        base = [p * reach + e * rows for p in range(bands)]
        for start in base:
            fill(start + 4, rows)
        conv_one([start + 2 for start in base], rows)

        @pl.when((lat == nlat - 1) & (e == steps - 1))
        def _():
            fn[height + 1 :] = nothing
            ff[height + 1 :] = nothing

        lhs = jnp.concatenate(
            [
                jnp.concatenate(
                    [buf[pl.ds(start + a, rows)].reshape(rows * half, 2 * c) for start in base], axis=0
                )
                for a in range(3)
                for buf in (fn, ff)
            ],
            axis=1,
        )
        second = jax.nn.gelu(dot(lhs, w2_ref[...])).astype(BF16)
        second = second.reshape(bands * UNIT, 2, half, 2 * c)
        patches = jnp.concatenate(
            [second[:, d].reshape(bands * UNIT * half, 2 * c) for d in range(2)], axis=1
        )
        coarse = dot(patches, mw_ref[...]).astype(BF16).reshape(bands, UNIT, half, latent)
        span = offset_lon // joint
        for u in range(UNIT):
            moved = dot(outward, coarse[:, u].reshape(cells, latent))
            sbuf[pl.ds(e * block + u * span, span)] = moved.reshape(span, joint * tokens, latent).astype(BF16)

        def send(k, carry):
            entry = e * block + (me + k) % block

            @pl.when(entry % count != me)
            def _():
                forward(entry).start()

            @pl.when(entry % count == me)
            def _():
                rbuf[pl.ds(entry, 1)] = sbuf[pl.ds(entry, 1)]

            return carry

        lax.fori_loop(1, block + 1, send, 0)
        return carry

    lax.fori_loop(0, steps, encode, 0)

    for load in loads[4:]:
        load.wait()

    def all_of(buffer, landing, send_sem, recv_sem, g):
        return pltpu.make_async_remote_copy(
            src_ref=buffer.at[pl.ds(0, count - 1)], dst_ref=landing.at[pl.ds(0, count - 1)],
            send_sem=send_sem.at[g], recv_sem=recv_sem.at[g],
            device_id=(lat, (lon + 1) % nlon), device_id_type=MESH,
        )

    def attend(g, carry):
        all_of(sbuf, rbuf, go_send, go_recv, g).wait_recv()
        at = pl.ds(g * count, count)
        cells_in = rbuf[at].astype(F32).reshape(count * joint * tokens, latent)
        total = window_block(joint, count, tokens, cells_in, g_ref, ai_ref, ao_ref, di_ref, do_ref)
        s2buf[at] = total.reshape(count, joint * tokens, latent).astype(BF16)

        def send(k, carry):
            peer = (me + k) % count
            pltpu.make_async_remote_copy(
                src_ref=s2buf.at[pl.ds(g * count + peer, 1)], dst_ref=r2buf.at[pl.ds(g * count + me, 1)],
                send_sem=back_send.at[g], recv_sem=back_recv.at[g],
                device_id=(peer // nlon, peer % nlon), device_id_type=MESH,
            ).start()
            return carry

        lax.fori_loop(1, count, send, 0)
        own = pl.ds(g * count + me, 1)
        r2buf[own] = s2buf[own]
        return carry

    lax.fori_loop(0, groups, attend, 0)

    per_group = steps // groups

    def expand(g, carry):
        all_of(s2buf, r2buf, back_send, back_recv, g).wait_recv()
        for k in range(per_group):
            e = g * per_group + k
            span = offset_lon // joint
            placed = []
            for u in range(UNIT):
                got = r2buf[pl.ds(e * block + u * span, span)].astype(F32).reshape(cells, latent)
                placed.append(dot(inward, got.astype(BF16)).astype(BF16))
            made = dot(jnp.concatenate(placed, axis=0), ew_ref[...])
            for u in range(UNIT):
                for p in range(bands):
                    top = u * cells + p * half
                    for d in range(4):
                        line = (p * rows + 2 * u + d // 2) * breadth + d % 2
                        os[pl.ds(line, half, stride=2), :] = made[top : top + half, d * c : (d + 1) * c]
            for p in range(bands):
                place = pl.ds(p * reach + e * rows, rows)
                lines = os[p * rows * breadth : (p + 1) * rows * breadth, :].reshape(rows, breadth, c)
                ost[place] = (lines + xv[place].astype(F32)).astype(BF16)
                pltpu.make_async_copy(ost.at[place], out_hbm.at[place], out_sem).start()
        return carry

    lax.fori_loop(0, groups, expand, 0)

    def settle(g, carry):
        all_of(sbuf, rbuf, go_send, go_recv, g).wait_send()
        all_of(s2buf, r2buf, back_send, back_recv, g).wait_send()
        return carry

    lax.fori_loop(0, groups, settle, 0)
    for _, _, there, _, copy in halo:
        pl.when(there)(copy.wait_send)
    pltpu.make_async_copy(ost, out_hbm, out_sem).wait()


def per_device(
    input_field,
    conv_one,
    conv_two,
    merge_weight,
    norm_gains,
    attention_in,
    attention_out,
    dense_in,
    dense_out,
    expand_weight,
):
    height, breadth, c = input_field.shape
    latent = merge_weight.shape[1]
    nlat = lax.axis_size("lat")
    nlon = lax.axis_size("lon")
    count = nlat * nlon
    bands = WINDOW // nlat
    per_lon = WINDOW // nlon
    offset_lat = height // (2 * bands)
    offset_lon = breadth // (2 * per_lon)
    tokens = bands * per_lon
    joint = max(1, 8 // tokens)
    entries = offset_lat * offset_lon // joint
    groups = entries // count
    half = breadth // 2
    pairs = -(-(half + 1) // 16) * 16
    pitch = -(-(LEAD + 2 * pairs) // 8) * 8
    rows = 2 * UNIT
    args = (
        input_field, conv_one, conv_two, merge_weight, norm_gains,
        attention_in, attention_out, dense_in, dense_out, expand_weight,
    )
    geo = (nlat, nlon, bands, per_lon, offset_lat, offset_lon, pairs, joint, groups)
    message = (entries, joint * tokens, latent)
    scratch = [pltpu.VMEM(a.shape, a.dtype) for a in args]
    scratch += [
        pltpu.VMEM((12 * c, 2 * c), BF16),
        pltpu.VMEM((12 * c, 2 * c), BF16),
        pltpu.VMEM(((height + 4) * pitch, c), F32),
        pltpu.VMEM((height + 4, pairs, 2 * c), BF16),
        pltpu.VMEM((height + 4, pairs, 2 * c), BF16),
        pltpu.VMEM((bands * rows, pairs, 2 * c), F32),
        pltpu.VMEM((height + 2, half, 2 * c), BF16),
        pltpu.VMEM((height + 2, half, 2 * c), BF16),
        pltpu.VMEM((2, height, 2 * c), BF16),
        pltpu.VMEM((2, height, 2 * c), BF16),
        pltpu.VMEM((2, 2, breadth, c), BF16),
        pltpu.VMEM((4, 16, 2 * c), BF16),
        pltpu.VMEM(message, BF16),
        pltpu.VMEM(message, BF16),
        pltpu.VMEM(message, BF16),
        pltpu.VMEM(message, BF16),
        pltpu.VMEM((bands * rows * breadth, c), F32),
        pltpu.VMEM((height, breadth, c), BF16),
        pltpu.SemaphoreType.DMA((10,)),
        pltpu.SemaphoreType.DMA((8,)),
        pltpu.SemaphoreType.DMA((8,)),
        pltpu.SemaphoreType.DMA((groups,)),
        pltpu.SemaphoreType.DMA((groups,)),
        pltpu.SemaphoreType.DMA((groups,)),
        pltpu.SemaphoreType.DMA((groups,)),
        pltpu.SemaphoreType.DMA,
    ]
    return pl.pallas_call(
        functools.partial(whole_body, geo),
        in_specs=[pl.BlockSpec(memory_space=pl.ANY)] * len(args),
        out_specs=pl.BlockSpec(memory_space=pl.ANY),
        out_shape=jax.ShapeDtypeStruct(input_field.shape, BF16),
        scratch_shapes=scratch,
        compiler_params=pltpu.CompilerParams(
            collective_id=0, has_side_effects=True, vmem_limit_bytes=LIMIT
        ),
        cost_estimate=pl.CostEstimate(flops=40_000_000_000, bytes_accessed=16_000_000, transcendentals=0),
        name="whole",
    )(*args)


def solution(mesh):
    return jax.shard_map(
        per_device,
        mesh=mesh,
        in_specs=(P("lat", "lon", None), P(), P(), P(), P(), P(), P(), P(), P(), P()),
        out_specs=P("lat", "lon", None),
        check_vma=False,
    )
```

time: 166 us -> 111 us (0.67)
  waiting for transfers between devices: 55.7 us -> 0 us
  Pallas kernels: 77.9 us -> 107 us
  starting transfers between devices: 24.4 us -> 0 us
  other arithmetic: 3.47 us -> 0 us
    all_to_all x4 -> x0, waiting for transfers between devices: 50.1 us -> none  [exchange(): lax.all_to_all(cells.reshape(devices, windows * tokens, latent), ('lat',...]
    pallas_call x6 -> x1, Pallas kernels: 77.9 us -> 107 us  [per_device(): pl.pallas_call(functools.partial(whole_body, geo), in_specs=[pl.BlockSpec...]
    all_to_all x4 -> x0, starting transfers between devices: 15.7 us -> none  [exchange(): lax.all_to_all(cells.reshape(devices, windows * tokens, latent), ('lat',...]
    ppermute x4 -> x0, starting transfers between devices: 8.74 us -> none  [the longest x2 6.15 us: padded(): lax.ppermute(tail, axis, [(i, (i + 1) % count) for i in range(ends)])]
    ppermute x4 -> x0, waiting for transfers between devices: 5.66 us -> none  [the longest x2 5.38 us: padded(): lax.ppermute(head, axis, [((i + 1) % count, i) for i in range(ends)])]
    concatenate x1 -> x0, other arithmetic: 2.87 us -> none  [padded(): jnp.concatenate([lax.ppermute(tail, axis, [(i, (i + 1) % count) for i in...]
  transfers between devices with their start and end apart: 8 -> 0, of which waited for: 7 -> 0; matrix products, arithmetic and copies ran while one was open for 2% -> 0% of each run, Pallas kernels for 36% -> 0%
where the time goes in v1:
time: 111 us; the launch traced here: 110 us
  Pallas kernels  107 us (96%)
  local copies, waits for them, and re-layouts  3.08 us (3%)
    pallas_call x1, Pallas kernels, per_device(): pl.pallas_call(functools.partial(whole_body, geo), in_specs=[pl.BlockSpec...  107 us
    unnamed x1, local copies, waits for them, and re-layouts  3.08 us

profile of v1, /device:TPU:0, one launch (start us, length us, event | category | flops | bytes accessed | tf_op | source)
XLA Modules:
  0.0 110.4 jit_solution(10272011509891488617)
XLA Ops:
  0.0 107.3 %whole.1 = bf16[128,64,128]{2,1,0:T(8,128)(2,1)} custom-call(bf16[128,64,128]{2,1,0:T(8,128)(2,1)} %x_hbm.1, bf16[3,3,128,128]{3,2,1,0:T(8,128)(2,1)} %k1_hbm.1, bf16[3,3,128,128]{3,2,1,0:T(8,128)(2,1)} %k2_hbm.1, bf16[512,512]{1,0:T(8,128)(2,1)} %mw_hbm.1, f32[4,512]{1,0:T(4,128)} %g_hbm.1, bf16[512,1536]{1,0:T(8,128)(2,1)} %ai_hbm.1, ...), custom_call_target="tpu_custom_call" | custom-call | flops 40000000000 | bytes 16000000 | tf_op jit(solution)/shard_map/whole/pallas_call | solution.py:476
  107.3 3.1 %copy.12 = bf16[128,64,128]{2,1,0:T(8,128)(2,1)} copy(bf16[128,64,128]{2,1,0:T(8,128)(2,1)} %whole.1) | data formatting | bytes 4194304

commit v2 on v1

--- a/solution.py
+++ b/solution.py
@@ -14,10 +14,12 @@
 FLOOR = 0.75
 F32 = jnp.float32
 BF16 = jnp.bfloat16
-LIMIT = 60 * 1024 * 1024
+LIMIT = 56 * 1024 * 1024
 MESH = pl.DeviceIdType.MESH
 LEAD = 8
 UNIT = 2
+EARLY = 2
+EARLY_AT = 1
 
 
 def dot(a, b):
@@ -112,11 +114,11 @@
     return total
 
 
-def whole_body(geo, x_hbm, k1_hbm, k2_hbm, mw_hbm, g_hbm, ai_hbm, ao_hbm, di_hbm, do_hbm, ew_hbm, out_hbm,
+def whole_body(geo, x_hbm, k1_hbm, k2_hbm, mw_hbm, g_hbm, ai_hbm, ao_hbm, di_hbm, do_hbm, ew_hbm, ost,
                xv, k1_ref, k2_ref, mw_ref, g_ref, ai_ref, ao_ref, di_ref, do_ref, ew_ref,
                w1_ref, w2_ref, xs, xn, xf, fs, fn, ff, edges, sides, caps, corners,
-               sbuf, rbuf, s2buf, r2buf, os, ost,
-               load_sem, halo_send, halo_recv, go_send, go_recv, back_send, back_recv, out_sem):
+               sbuf, rbuf, s2buf, r2buf, os,
+               load_sem, halo_send, halo_recv, go_send, go_recv, back_send, back_recv):
     (nlat, nlon, bands, per_lon, offset_lat, offset_lon, pairs, joint, groups) = geo
     count = nlat * nlon
     lat = lax.axis_index("lat")
@@ -133,25 +135,31 @@
     block = UNIT * offset_lon // joint
     pitch = xs.shape[0] // (height + 4)
 
-    barrier = pltpu.get_barrier_semaphore()
-
-    def greet(k, carry):
-        peer = (me + k) % count
-        pl.semaphore_signal(barrier, inc=1, device_id=(peer // nlon, peer % nlon), device_id_type=MESH)
-        return carry
-
-    lax.fori_loop(1, count, greet, 0)
-
-    loads = [
-        pltpu.make_async_copy(a, b, load_sem.at[i])
-        for i, (a, b) in enumerate(
-            [(x_hbm, xv), (k1_hbm, k1_ref), (k2_hbm, k2_ref), (mw_hbm, mw_ref), (g_hbm, g_ref),
-             (ai_hbm, ai_ref), (ao_hbm, ao_ref), (di_hbm, di_ref), (do_hbm, do_ref), (ew_hbm, ew_ref)]
-        )
+    head = EARLY_AT * rows - 2
+    depth = rows + 4
+    firsts = [pl.ds(p * reach + head, depth) for p in range(bands)]
+    stops = [0] + [p * reach + head + depth for p in range(bands)]
+    rests = [
+        pl.ds(stop, (p * reach + head if p < bands else height) - stop) for p, stop in enumerate(stops)
     ]
+    pieces = [(x_hbm.at[at], xv.at[at]) for at in firsts]
+    pieces += [(k1_hbm, k1_ref), (k2_hbm, k2_ref), (mw_hbm, mw_ref)]
+    pieces += [(x_hbm.at[at], xv.at[at]) for at in rests]
+    pieces += [(g_hbm, g_ref), (ai_hbm, ai_ref), (ao_hbm, ao_ref), (di_hbm, di_ref), (do_hbm, do_ref), (ew_hbm, ew_ref)]
+    loads = [pltpu.make_async_copy(a, b, load_sem.at[i]) for i, (a, b) in enumerate(pieces)]
     for load in loads:
         load.start()
-    loads[0].wait()
+
+    barrier = pltpu.get_barrier_semaphore()
+
+    def greet(k, carry):
+        peer = lax.rem(me + k, count)
+        pl.semaphore_signal(
+            barrier, inc=1, device_id=(lax.div(peer, nlon), lax.rem(peer, nlon)), device_id_type=MESH
+        )
+        return carry
+
+    lax.fori_loop(1, count, greet, 0)
 
     def widen(r, carry):
         for k in range(4):
@@ -159,15 +167,132 @@
             xs[pl.ds((at + 2) * pitch + LEAD, breadth), :] = xv[at].astype(F32)
         return carry
 
-    lax.fori_loop(0, height // 4, widen, 0)
-
     def column(at):
         return xs[pl.ds(2 * pitch + LEAD + at, height, stride=pitch), :]
 
+    left, right = LEAD - 2, LEAD + breadth
+    for col in (left, left + 1, right, right + 1):
+        xs[pl.ds(col, height + 4, stride=pitch), :] = jnp.zeros((height + 4, c), F32)
+
+    for p in range(bands):
+        loads[p].wait()
+        for r in range(depth):
+            at = p * reach + head + r
+            xs[pl.ds((at + 2) * pitch + LEAD, breadth), :] = xv[at].astype(F32)
+    loads[bands].wait()
+    pair_kernel(k1_ref, w1_ref)
+    loads[bands + 1].wait()
+    pair_kernel(k2_ref, w2_ref)
+    loads[bands + 2].wait()
+
+    def fill(start, n):
+        for r in range(n):
+            base = (start + r) * pitch + left
+            quad = [xs[pl.ds(base + j, pairs, stride=2), :] for j in range(4)]
+            xn[pl.ds(start + r, 1)] = jnp.concatenate(quad[:2], axis=1).astype(BF16)[None]
+            xf[pl.ds(start + r, 1)] = jnp.concatenate(quad[2:], axis=1).astype(BF16)[None]
+
+    pair = lax.broadcasted_iota(jnp.int32, (pairs, 2 * c), 0)
+    lane = lax.broadcasted_iota(jnp.int32, (pairs, 2 * c), 1)
+    lon_place = 2 * pair + (lane >= c).astype(jnp.int32) + (lon * breadth - 1)
+    inside = (lon_place >= 0) & (lon_place < nlon * breadth)
+
+    def conv_one(starts, n):
+        lhs = jnp.concatenate(
+            [
+                jnp.concatenate(
+                    [buf[pl.ds(start + a, n)].reshape(n * pairs, 2 * c) for start in starts], axis=0
+                )
+                for a in range(3)
+                for buf in (xn, xf)
+            ],
+            axis=1,
+        )
+        first = jax.nn.gelu(dot(lhs, w1_ref[...])).reshape(bands * n, pairs, 2 * c)
+        fs[: bands * n] = jnp.where(inside[None], first, 0.0)
+        for p, start in enumerate(starts):
+            fn[pl.ds(start, n)] = fs[p * n : (p + 1) * n, 0:half, :].astype(BF16)
+            ff[pl.ds(start, n)] = fs[p * n : (p + 1) * n, pl.ds(1, half), :].astype(BF16)
+
+    to = lax.broadcasted_iota(jnp.int32, (cells, cells), 0)
+    of = lax.broadcasted_iota(jnp.int32, (cells, cells), 1)
+    outward = ones_where(of == (to % tokens) * offset_lon + to // tokens)
+    inward = ones_where(of == (to % offset_lon) * tokens + to // offset_lon)
+
+    span = offset_lon // joint
+    nothing = jnp.zeros((1, half, 2 * c), BF16)
+
+    def forward(entry, source):
+        peer = lax.rem(entry, count)
+        group = lax.div(entry, count)
+        return pltpu.make_async_remote_copy(
+            src_ref=sbuf.at[pl.ds(source, 1)], dst_ref=rbuf.at[pl.ds(group * count + me, 1)],
+            send_sem=go_send.at[group], recv_sem=go_recv.at[group],
+            device_id=(lax.div(peer, nlon), lax.rem(peer, nlon)), device_id_type=MESH,
+        )
+
+    def tail(base, place):
+        lhs = jnp.concatenate(
+            [
+                jnp.concatenate(
+                    [buf[pl.ds(start + a, rows)].reshape(rows * half, 2 * c) for start in base], axis=0
+                )
+                for a in range(3)
+                for buf in (fn, ff)
+            ],
+            axis=1,
+        )
+        second = jax.nn.gelu(dot(lhs, w2_ref[...])).astype(BF16)
+        second = second.reshape(bands * UNIT, 2, half, 2 * c)
+        patches = jnp.concatenate(
+            [second[:, d].reshape(bands * UNIT * half, 2 * c) for d in range(2)], axis=1
+        )
+        coarse = dot(patches, mw_ref[...]).astype(BF16).reshape(bands, UNIT, half, latent)
+        for u in range(UNIT):
+            moved = dot(outward, coarse[:, u].reshape(cells, latent))
+            sbuf[pl.ds(place + u * span, span)] = moved.reshape(span, joint * tokens, latent).astype(BF16)
+
+
+    def post(e, place, chosen):
+        def send(k, carry):
+            i = lax.rem(me + k, block)
+            entry = e * block + i
+            spot = lax.rem(i, span)
+            take = chosen((spot == 0) | (spot == span - 1))
+            mine = lax.rem(entry, count) == me
+
+            @pl.when(take & jnp.logical_not(mine))
+            def _():
+                forward(entry, place + i).start()
+
+            @pl.when(take & mine)
+            def _():
+                rbuf[pl.ds(entry, 1)] = sbuf[pl.ds(place + i, 1)]
+
+            return carry
+
+        lax.fori_loop(1, block + 1, send, 0)
+
+    def early(j):
+        e = EARLY_AT + j
+        base = [p * reach + e * rows for p in range(bands)]
+        for start in base:
+            fill(start, rows + 4)
+        conv_one(base, rows + 2)
+        tail(base, (steps + j) * block)
+
+    def early_post(j):
+        post(EARLY_AT + j, (steps + j) * block, jnp.logical_not)
+
+    early(0)
+    pl.semaphore_wait(barrier, count - 1)
+    early_post(0)
+
+    for load in loads[bands + 3 : 2 * bands + 4]:
+        load.wait()
+    lax.fori_loop(0, height // 4, widen, 0)
     for side, at in enumerate((0, breadth - 2)):
         edges[side] = jnp.concatenate([column(at), column(at + 1)], axis=1).astype(BF16)
-
-    pl.semaphore_wait(barrier, count - 1)
 
     tip = 16
     ends = (slice(0, tip), slice(height - tip, height))
@@ -192,13 +317,10 @@
         halo.append((dy, dx, there, back, copy))
         pl.when(there)(copy.start)
 
-    loads[1].wait()
-    pair_kernel(k1_ref, w1_ref)
-    loads[2].wait()
-    pair_kernel(k2_ref, w2_ref)
-    loads[3].wait()
-
-    left, right = LEAD - 2, LEAD + breadth
+    for j in range(1, EARLY):
+        early(j)
+        early_post(j)
+
     for dy, dx, there, back, copy in halo:
         row = 0 if dy > 0 else height + 2
         col = left if dx > 0 else right
@@ -221,75 +343,29 @@
                             base + r : base + r + 1, k * c : (k + 1) * c
                         ]
 
-        def empty(dy=dy, dx=dx, row=row, col=col):
-            if dx == 0:
-                for k in range(2):
-                    xs[pl.ds((row + k) * pitch + LEAD, breadth), :] = jnp.zeros((breadth, c), F32)
-            elif dy == 0:
-                for k in range(2):
-                    xs[pl.ds(2 * pitch + col + k, height, stride=pitch), :] = jnp.zeros((height, c), F32)
-            else:
-                for r in range(2):
-                    for k in range(2):
-                        xs[pl.ds((row + r) * pitch + col + k, 1), :] = jnp.zeros((1, c), F32)
+        def empty(row=row):
+            for k in range(2):
+                xs[pl.ds((row + k) * pitch + LEAD, breadth), :] = jnp.zeros((breadth, c), F32)
 
         pl.when(back)(landed)
-        pl.when(jnp.logical_not(back))(empty)
-
-    def fill(start, n):
-        for r in range(n):
-            base = (start + r) * pitch + left
-            quad = [xs[pl.ds(base + j, pairs, stride=2), :] for j in range(4)]
-            xn[pl.ds(start + r, 1)] = jnp.concatenate(quad[:2], axis=1).astype(BF16)[None]
-            xf[pl.ds(start + r, 1)] = jnp.concatenate(quad[2:], axis=1).astype(BF16)[None]
-
-    pair = lax.broadcasted_iota(jnp.int32, (pairs, 2 * c), 0)
-    lane = lax.broadcasted_iota(jnp.int32, (pairs, 2 * c), 1)
-    lon_place = 2 * pair + (lane >= c).astype(jnp.int32) + (lon * breadth - 1)
-    inside = (lon_place >= 0) & (lon_place < nlon * breadth)
-
-    def conv_one(starts, n):
-        lhs = jnp.concatenate(
-            [
-                jnp.concatenate(
-                    [buf[pl.ds(start + a, n)].reshape(n * pairs, 2 * c) for start in starts], axis=0
-                )
-                for a in range(3)
-                for buf in (xn, xf)
-            ],
-            axis=1,
-        )
-        first = jax.nn.gelu(dot(lhs, w1_ref[...])).reshape(bands * n, pairs, 2 * c)
-        fs[: bands * n] = jnp.where(inside[None], first, 0.0)
-        for p, start in enumerate(starts):
-            fn[pl.ds(start, n)] = fs[p * n : (p + 1) * n, 0:half, :].astype(BF16)
-            ff[pl.ds(start, n)] = fs[p * n : (p + 1) * n, pl.ds(1, half), :].astype(BF16)
-
-    nothing = jnp.zeros((1, half, 2 * c), BF16)
-    for p in range(bands):
-        fill(p * reach, 4)
-    conv_one([p * reach for p in range(bands)], 2)
-
-    @pl.when(lat == 0)
-    def _():
-        fn[0:1] = nothing
-        ff[0:1] = nothing
-
-    to = lax.broadcasted_iota(jnp.int32, (cells, cells), 0)
-    of = lax.broadcasted_iota(jnp.int32, (cells, cells), 1)
-    outward = ones_where(of == (to % tokens) * offset_lon + to // tokens)
-    inward = ones_where(of == (to % offset_lon) * tokens + to // offset_lon)
-
-    def forward(entry):
-        peer = entry % count
-        return pltpu.make_async_remote_copy(
-            src_ref=sbuf.at[pl.ds(entry, 1)], dst_ref=rbuf.at[pl.ds(entry // count * count + me, 1)],
-            send_sem=go_send.at[entry // count], recv_sem=go_recv.at[entry // count],
-            device_id=(peer // nlon, peer % nlon), device_id_type=MESH,
-        )
-
-    def encode(e, carry):
+        if dx == 0:
+            pl.when(jnp.logical_not(back))(empty)
+
+    def encode(k, carry):
+        e = lax.rem(k + EARLY_AT + EARLY, steps)
         base = [p * reach + e * rows for p in range(bands)]
+
+        @pl.when((k == 0) | (e == 0))
+        def _():
+            for start in base:
+                fill(start, 4)
+            conv_one(base, 2)
+
+        @pl.when((lat == 0) & (e == 0))
+        def _():
+            fn[0:1] = nothing
+            ff[0:1] = nothing
+
         for start in base:
             fill(start + 4, rows)
         conv_one([start + 2 for start in base], rows)
@@ -299,46 +375,14 @@
             fn[height + 1 :] = nothing
             ff[height + 1 :] = nothing
 
-        lhs = jnp.concatenate(
-            [
-                jnp.concatenate(
-                    [buf[pl.ds(start + a, rows)].reshape(rows * half, 2 * c) for start in base], axis=0
-                )
-                for a in range(3)
-                for buf in (fn, ff)
-            ],
-            axis=1,
-        )
-        second = jax.nn.gelu(dot(lhs, w2_ref[...])).astype(BF16)
-        second = second.reshape(bands * UNIT, 2, half, 2 * c)
-        patches = jnp.concatenate(
-            [second[:, d].reshape(bands * UNIT * half, 2 * c) for d in range(2)], axis=1
-        )
-        coarse = dot(patches, mw_ref[...]).astype(BF16).reshape(bands, UNIT, half, latent)
-        span = offset_lon // joint
-        for u in range(UNIT):
-            moved = dot(outward, coarse[:, u].reshape(cells, latent))
-            sbuf[pl.ds(e * block + u * span, span)] = moved.reshape(span, joint * tokens, latent).astype(BF16)
-
-        def send(k, carry):
-            entry = e * block + (me + k) % block
-
-            @pl.when(entry % count != me)
-            def _():
-                forward(entry).start()
-
-            @pl.when(entry % count == me)
-            def _():
-                rbuf[pl.ds(entry, 1)] = sbuf[pl.ds(entry, 1)]
-
-            return carry
-
-        lax.fori_loop(1, block + 1, send, 0)
+        tail(base, e * block)
+        fresh = (e < EARLY_AT) | (e >= EARLY_AT + EARLY)
+        post(e, e * block, lambda edge: edge | fresh)
         return carry
 
     lax.fori_loop(0, steps, encode, 0)
 
-    for load in loads[4:]:
+    for load in loads[2 * bands + 4 :]:
         load.wait()
 
     def all_of(buffer, landing, send_sem, recv_sem, g):
@@ -348,7 +392,11 @@
             device_id=(lat, (lon + 1) % nlon), device_id_type=MESH,
         )
 
-    def attend(g, carry):
+    per_group = steps // groups
+    ahead = -(-(EARLY_AT + EARLY) // per_group)
+
+    def attend(k, carry):
+        g = lax.rem(k + ahead, groups)
         all_of(sbuf, rbuf, go_send, go_recv, g).wait_recv()
         at = pl.ds(g * count, count)
         cells_in = rbuf[at].astype(F32).reshape(count * joint * tokens, latent)
@@ -356,11 +404,11 @@
         s2buf[at] = total.reshape(count, joint * tokens, latent).astype(BF16)
 
         def send(k, carry):
-            peer = (me + k) % count
+            peer = lax.rem(me + k, count)
             pltpu.make_async_remote_copy(
                 src_ref=s2buf.at[pl.ds(g * count + peer, 1)], dst_ref=r2buf.at[pl.ds(g * count + me, 1)],
                 send_sem=back_send.at[g], recv_sem=back_recv.at[g],
-                device_id=(peer // nlon, peer % nlon), device_id_type=MESH,
+                device_id=(lax.div(peer, nlon), lax.rem(peer, nlon)), device_id_type=MESH,
             ).start()
             return carry
 
@@ -371,13 +419,11 @@
 
     lax.fori_loop(0, groups, attend, 0)
 
-    per_group = steps // groups
-
-    def expand(g, carry):
+    def expand(i, carry):
+        g = lax.rem(i + ahead, groups)
         all_of(s2buf, r2buf, back_send, back_recv, g).wait_recv()
         for k in range(per_group):
             e = g * per_group + k
-            span = offset_lon // joint
             placed = []
             for u in range(UNIT):
                 got = r2buf[pl.ds(e * block + u * span, span)].astype(F32).reshape(cells, latent)
@@ -393,7 +439,6 @@
                 place = pl.ds(p * reach + e * rows, rows)
                 lines = os[p * rows * breadth : (p + 1) * rows * breadth, :].reshape(rows, breadth, c)
                 ost[place] = (lines + xv[place].astype(F32)).astype(BF16)
-                pltpu.make_async_copy(ost.at[place], out_hbm.at[place], out_sem).start()
         return carry
 
     lax.fori_loop(0, groups, expand, 0)
@@ -406,7 +451,6 @@
     lax.fori_loop(0, groups, settle, 0)
     for _, _, there, _, copy in halo:
         pl.when(there)(copy.wait_send)
-    pltpu.make_async_copy(ost, out_hbm, out_sem).wait()
 
 
 def per_device(
@@ -438,6 +482,7 @@
     pairs = -(-(half + 1) // 16) * 16
     pitch = -(-(LEAD + 2 * pairs) // 8) * 8
     rows = 2 * UNIT
+    block = UNIT * offset_lon // joint
     args = (
         input_field, conv_one, conv_two, merge_weight, norm_gains,
         attention_in, attention_out, dense_in, dense_out, expand_weight,
@@ -451,33 +496,31 @@
         pltpu.VMEM(((height + 4) * pitch, c), F32),
         pltpu.VMEM((height + 4, pairs, 2 * c), BF16),
         pltpu.VMEM((height + 4, pairs, 2 * c), BF16),
-        pltpu.VMEM((bands * rows, pairs, 2 * c), F32),
+        pltpu.VMEM((bands * (rows + 2), pairs, 2 * c), F32),
         pltpu.VMEM((height + 2, half, 2 * c), BF16),
         pltpu.VMEM((height + 2, half, 2 * c), BF16),
         pltpu.VMEM((2, height, 2 * c), BF16),
         pltpu.VMEM((2, height, 2 * c), BF16),
         pltpu.VMEM((2, 2, breadth, c), BF16),
         pltpu.VMEM((4, 16, 2 * c), BF16),
-        pltpu.VMEM(message, BF16),
+        pltpu.VMEM((entries + EARLY * block,) + message[1:], BF16),
         pltpu.VMEM(message, BF16),
         pltpu.VMEM(message, BF16),
         pltpu.VMEM(message, BF16),
         pltpu.VMEM((bands * rows * breadth, c), F32),
-        pltpu.VMEM((height, breadth, c), BF16),
-        pltpu.SemaphoreType.DMA((10,)),
+        pltpu.SemaphoreType.DMA((2 * bands + 10,)),
         pltpu.SemaphoreType.DMA((8,)),
         pltpu.SemaphoreType.DMA((8,)),
         pltpu.SemaphoreType.DMA((groups,)),
         pltpu.SemaphoreType.DMA((groups,)),
         pltpu.SemaphoreType.DMA((groups,)),
         pltpu.SemaphoreType.DMA((groups,)),
-        pltpu.SemaphoreType.DMA,
     ]
     return pl.pallas_call(
         functools.partial(whole_body, geo),
         in_specs=[pl.BlockSpec(memory_space=pl.ANY)] * len(args),
-        out_specs=pl.BlockSpec(memory_space=pl.ANY),
-        out_shape=jax.ShapeDtypeStruct(input_field.shape, BF16),
+        out_specs=pl.BlockSpec(memory_space=pltpu.VMEM),
+        out_shape=pltpu.VMEM(input_field.shape, BF16),
         scratch_shapes=scratch,
         compiler_params=pltpu.CompilerParams(
             collective_id=0, has_side_effects=True, vmem_limit_bytes=LIMIT

time: 111 us -> 104 us (0.937)
  Pallas kernels: 107 us -> 102 us
  local copies, waits for them, and re-layouts: 3.08 us -> 1.32 us
    pallas_call x1, Pallas kernels: 107 us -> 102 us  [per_device(): pl.pallas_call(functools.partial(whole_body, geo), in_specs=[pl.BlockSpec...]
    unnamed x1, local copies, waits for them, and re-layouts: 3.08 us -> 1.32 us
where the time goes in v2:
time: 104 us
  Pallas kernels  102 us (98%)
  local copies, waits for them, and re-layouts  1.32 us (1%)
    pallas_call x1, Pallas kernels, per_device(): pl.pallas_call(functools.partial(whole_body, geo), in_specs=[pl.BlockSpec...  102 us

profile of v2, /device:TPU:0, one launch (start us, length us, event | category | flops | bytes accessed | tf_op | source)
XLA Modules:
  0.0 103.7 jit_solution(10375868651407031366)
XLA Ops:
  0.0 102.4 %whole.1 = bf16[128,64,128]{2,1,0:T(8,128)(2,1)S(1)} custom-call(bf16[128,64,128]{2,1,0:T(8,128)(2,1)} %x_hbm.1, bf16[3,3,128,128]{3,2,1,0:T(8,128)(2,1)} %k1_hbm.1, bf16[3,3,128,128]{3,2,1,0:T(8,128)(2,1)} %k2_hbm.1, bf16[512,512]{1,0:T(8,128)(2,1)} %mw_hbm.1, f32[4,512]{1,0:T(4,128)} %g_hbm.1, bf16[512,1536]{1,0:T(8,128)(2,1)} %ai_hbm.1, ...), custom_call_target="tpu_custom_call" | custom-call | flops 40000000000 | bytes 16000000 | tf_op jit(solution)/shard_map/whole/pallas_call | solution.py:519
  102.4 1.3 %copy.12 = bf16[128,64,128]{2,1,0:T(8,128)(2,1)} copy(bf16[128,64,128]{2,1,0:T(8,128)(2,1)S(1)} %whole.1) | data formatting | bytes 4194304

commit v3 on v2

--- a/solution.py
+++ b/solution.py
@@ -16,6 +16,7 @@
 BF16 = jnp.bfloat16
 LIMIT = 56 * 1024 * 1024
 MESH = pl.DeviceIdType.MESH
+FLAT = pl.DeviceIdType.LOGICAL
 LEAD = 8
 UNIT = 2
 EARLY = 2
@@ -153,10 +154,7 @@
     barrier = pltpu.get_barrier_semaphore()
 
     def greet(k, carry):
-        peer = lax.rem(me + k, count)
-        pl.semaphore_signal(
-            barrier, inc=1, device_id=(lax.div(peer, nlon), lax.rem(peer, nlon)), device_id_type=MESH
-        )
+        pl.semaphore_signal(barrier, inc=1, device_id=lax.rem(me + k, count), device_id_type=FLAT)
         return carry
 
     lax.fori_loop(1, count, greet, 0)
@@ -222,20 +220,12 @@
     span = offset_lon // joint
     nothing = jnp.zeros((1, half, 2 * c), BF16)
 
-    def forward(entry, source):
-        peer = lax.rem(entry, count)
-        group = lax.div(entry, count)
-        return pltpu.make_async_remote_copy(
-            src_ref=sbuf.at[pl.ds(source, 1)], dst_ref=rbuf.at[pl.ds(group * count + me, 1)],
-            send_sem=go_send.at[group], recv_sem=go_recv.at[group],
-            device_id=(lax.div(peer, nlon), lax.rem(peer, nlon)), device_id_type=MESH,
-        )
-
-    def tail(base, place):
+    def tail(base, place, units):
+        lines = 2 * units
         lhs = jnp.concatenate(
             [
                 jnp.concatenate(
-                    [buf[pl.ds(start + a, rows)].reshape(rows * half, 2 * c) for start in base], axis=0
+                    [buf[pl.ds(start + a, lines)].reshape(lines * half, 2 * c) for start in base], axis=0
                 )
                 for a in range(3)
                 for buf in (fn, ff)
@@ -243,50 +233,60 @@
             axis=1,
         )
         second = jax.nn.gelu(dot(lhs, w2_ref[...])).astype(BF16)
-        second = second.reshape(bands * UNIT, 2, half, 2 * c)
+        second = second.reshape(bands * units, 2, half, 2 * c)
         patches = jnp.concatenate(
-            [second[:, d].reshape(bands * UNIT * half, 2 * c) for d in range(2)], axis=1
+            [second[:, d].reshape(bands * units * half, 2 * c) for d in range(2)], axis=1
         )
-        coarse = dot(patches, mw_ref[...]).astype(BF16).reshape(bands, UNIT, half, latent)
-        for u in range(UNIT):
+        coarse = dot(patches, mw_ref[...]).astype(BF16).reshape(bands, units, half, latent)
+        for u in range(units):
             moved = dot(outward, coarse[:, u].reshape(cells, latent))
             sbuf[pl.ds(place + u * span, span)] = moved.reshape(span, joint * tokens, latent).astype(BF16)
 
 
-    def post(e, place, chosen):
+    def post(e, place, low, n, chosen):
         def send(k, carry):
-            i = lax.rem(me + k, block)
+            i = low + lax.rem(me + k, n)
             entry = e * block + i
+            peer = i if block == count else lax.rem(entry, count)
+            group = e if block == count else lax.div(entry, count)
             spot = lax.rem(i, span)
             take = chosen((spot == 0) | (spot == span - 1))
-            mine = lax.rem(entry, count) == me
-
-            @pl.when(take & jnp.logical_not(mine))
+
+            @pl.when(take & (peer != me))
             def _():
-                forward(entry, place + i).start()
-
-            @pl.when(take & mine)
+                pltpu.make_async_remote_copy(
+                    src_ref=sbuf.at[pl.ds(place + i, 1)], dst_ref=rbuf.at[pl.ds(group * count + me, 1)],
+                    send_sem=go_send.at[group], recv_sem=go_recv.at[group],
+                    device_id=peer, device_id_type=FLAT,
+                ).start()
+
+            @pl.when(take & (peer == me))
             def _():
                 rbuf[pl.ds(entry, 1)] = sbuf[pl.ds(place + i, 1)]
 
             return carry
 
-        lax.fori_loop(1, block + 1, send, 0)
-
-    def early(j):
+        lax.fori_loop(1, n + 1, send, 0)
+
+    def early(j, low, units):
         e = EARLY_AT + j
-        base = [p * reach + e * rows for p in range(bands)]
+        base = [p * reach + e * rows + 2 * low for p in range(bands)]
+        fresh = j == 0 and low == 0
+        more = 2 if fresh else 0
         for start in base:
-            fill(start, rows + 4)
-        conv_one(base, rows + 2)
-        tail(base, (steps + j) * block)
-
-    def early_post(j):
-        post(EARLY_AT + j, (steps + j) * block, jnp.logical_not)
-
-    early(0)
+            fill(start + 4 - 2 * more, 2 * units + 2 * more)
+        conv_one([start + 2 - more for start in base], 2 * units + more)
+        tail(base, (steps + j) * block + low * span, units)
+
+    def early_post(j, low, units):
+        post(EARLY_AT + j, (steps + j) * block, low * span, units * span, jnp.logical_not)
+
+    early(0, 0, 1)
     pl.semaphore_wait(barrier, count - 1)
-    early_post(0)
+    early_post(0, 0, 1)
+    for low in range(1, UNIT):
+        early(0, low, 1)
+        early_post(0, low, 1)
 
     for load in loads[bands + 3 : 2 * bands + 4]:
         load.wait()
@@ -318,8 +318,8 @@
         pl.when(there)(copy.start)
 
     for j in range(1, EARLY):
-        early(j)
-        early_post(j)
+        early(j, 0, UNIT)
+        early_post(j, 0, UNIT)
 
     for dy, dx, there, back, copy in halo:
         row = 0 if dy > 0 else height + 2
@@ -375,9 +375,9 @@
             fn[height + 1 :] = nothing
             ff[height + 1 :] = nothing
 
-        tail(base, e * block)
+        tail(base, e * block, UNIT)
         fresh = (e < EARLY_AT) | (e >= EARLY_AT + EARLY)
-        post(e, e * block, lambda edge: edge | fresh)
+        post(e, e * block, 0, block, lambda edge: edge | fresh)
         return carry
 
     lax.fori_loop(0, steps, encode, 0)
@@ -408,7 +408,7 @@
             pltpu.make_async_remote_copy(
                 src_ref=s2buf.at[pl.ds(g * count + peer, 1)], dst_ref=r2buf.at[pl.ds(g * count + me, 1)],
                 send_sem=back_send.at[g], recv_sem=back_recv.at[g],
-                device_id=(lax.div(peer, nlon), lax.rem(peer, nlon)), device_id_type=MESH,
+                device_id=peer, device_id_type=FLAT,
             ).start()
             return carry
 

time: 104 us -> 103 us (level)
  no operation moved by 1% of the time
where the time goes in v3:
time: 103 us
  Pallas kernels  102 us (99%)
  local copies, waits for them, and re-layouts  1.32 us (1%)
    pallas_call x1, Pallas kernels, per_device(): pl.pallas_call(functools.partial(whole_body, geo), in_specs=[pl.BlockSpec...  102 us

profile of v3, /device:TPU:0, one launch (start us, length us, event | category | flops | bytes accessed | tf_op | source)
XLA Modules:
  0.0 103.1 jit_solution(5914945217739500739)
XLA Ops:
  0.0 101.8 %whole.1 = bf16[128,64,128]{2,1,0:T(8,128)(2,1)S(1)} custom-call(bf16[128,64,128]{2,1,0:T(8,128)(2,1)} %x_hbm.1, bf16[3,3,128,128]{3,2,1,0:T(8,128)(2,1)} %k1_hbm.1, bf16[3,3,128,128]{3,2,1,0:T(8,128)(2,1)} %k2_hbm.1, bf16[512,512]{1,0:T(8,128)(2,1)} %mw_hbm.1, f32[4,512]{1,0:T(4,128)} %g_hbm.1, bf16[512,1536]{1,0:T(8,128)(2,1)} %ai_hbm.1, ...), custom_call_target="tpu_custom_call" | custom-call | flops 40000000000 | bytes 16000000 | tf_op jit(solution)/shard_map/whole/pallas_call | solution.py:519
  101.8 1.3 %copy.12 = bf16[128,64,128]{2,1,0:T(8,128)(2,1)} copy(bf16[128,64,128]{2,1,0:T(8,128)(2,1)S(1)} %whole.1) | data formatting | bytes 4194304

commit v4 on v3

--- a/solution.py
+++ b/solution.py
@@ -19,6 +19,7 @@
 FLAT = pl.DeviceIdType.LOGICAL
 LEAD = 8
 UNIT = 2
+FLUSHES = 8
 EARLY = 2
 EARLY_AT = 1
 
@@ -134,7 +135,7 @@
     rows = 2 * UNIT
     steps = offset_lat // UNIT
     block = UNIT * offset_lon // joint
-    pitch = xs.shape[0] // (height + 4)
+    pitch = xs.shape[0] // (height + 5)
 
     head = EARLY_AT * rows - 2
     depth = rows + 4
@@ -451,6 +452,18 @@
     lax.fori_loop(0, groups, settle, 0)
     for _, _, there, _, copy in halo:
         pl.when(there)(copy.wait_send)
+
+
+def flush_body(made_ref, out_ref, sems):
+    share = made_ref.shape[0] // FLUSHES
+    copies = [
+        pltpu.make_async_copy(made_ref.at[pl.ds(i * share, share)], out_ref.at[pl.ds(i * share, share)], sems.at[i])
+        for i in range(FLUSHES)
+    ]
+    for copy in copies:
+        copy.start()
+    for copy in copies:
+        copy.wait()
 
 
 def per_device(
@@ -493,7 +506,7 @@
     scratch += [
         pltpu.VMEM((12 * c, 2 * c), BF16),
         pltpu.VMEM((12 * c, 2 * c), BF16),
-        pltpu.VMEM(((height + 4) * pitch, c), F32),
+        pltpu.VMEM(((height + 5) * pitch, c), F32),
         pltpu.VMEM((height + 4, pairs, 2 * c), BF16),
         pltpu.VMEM((height + 4, pairs, 2 * c), BF16),
         pltpu.VMEM((bands * (rows + 2), pairs, 2 * c), F32),
@@ -507,7 +520,7 @@
         pltpu.VMEM(message, BF16),
         pltpu.VMEM(message, BF16),
         pltpu.VMEM(message, BF16),
-        pltpu.VMEM((bands * rows * breadth, c), F32),
+        pltpu.VMEM((bands * rows * breadth + 8, c), F32),
         pltpu.SemaphoreType.DMA((2 * bands + 10,)),
         pltpu.SemaphoreType.DMA((8,)),
         pltpu.SemaphoreType.DMA((8,)),
@@ -516,7 +529,7 @@
         pltpu.SemaphoreType.DMA((groups,)),
         pltpu.SemaphoreType.DMA((groups,)),
     ]
-    return pl.pallas_call(
+    made = pl.pallas_call(
         functools.partial(whole_body, geo),
         in_specs=[pl.BlockSpec(memory_space=pl.ANY)] * len(args),
         out_specs=pl.BlockSpec(memory_space=pltpu.VMEM),
@@ -528,6 +541,16 @@
         cost_estimate=pl.CostEstimate(flops=40_000_000_000, bytes_accessed=16_000_000, transcendentals=0),
         name="whole",
     )(*args)
+    return pl.pallas_call(
+        flush_body,
+        in_specs=[pl.BlockSpec(memory_space=pltpu.VMEM)],
+        out_specs=pl.BlockSpec(memory_space=pl.ANY),
+        out_shape=jax.ShapeDtypeStruct(input_field.shape, BF16),
+        scratch_shapes=[pltpu.SemaphoreType.DMA((FLUSHES,))],
+        cost_estimate=pl.CostEstimate(flops=1_000_000, bytes_accessed=4_000_000, transcendentals=0),
+        compiler_params=pltpu.CompilerParams(vmem_limit_bytes=4 * 1024 * 1024),
+        name="flush",
+    )(made)
 
 
 def solution(mesh):

time: 103 us -> 103 us (level)
  local copies, waits for them, and re-layouts: 1.32 us -> 0 us
    pallas_call x0 -> x1, Pallas kernels: none -> 1.38 us  [per_device(): pl.pallas_call(flush_body, in_specs=[pl.BlockSpec(memory_space=pltpu.VMEM...]
    unnamed x1 -> x0, local copies, waits for them, and re-layouts: 1.32 us -> none
where the time goes in v4:
time: 103 us
  Pallas kernels  103 us (100%)
    pallas_call x1, Pallas kernels, per_device(): pl.pallas_call(functools.partial(whole_body, geo), in_specs=[pl.BlockSpec...  102 us

profile of v4, /device:TPU:0, one launch (start us, length us, event | category | flops | bytes accessed | tf_op | source)
XLA Modules:
  0.0 103.2 jit_solution(11354228429939208184)
XLA Ops:
  0.0 101.8 %whole.1.made_ref = bf16[128,64,128]{2,1,0:T(8,128)(2,1)S(1)} custom-call(bf16[128,64,128]{2,1,0:T(8,128)(2,1)} %x_hbm.1, bf16[3,3,128,128]{3,2,1,0:T(8,128)(2,1)} %k1_hbm.1, bf16[3,3,128,128]{3,2,1,0:T(8,128)(2,1)} %k2_hbm.1, bf16[512,512]{1,0:T(8,128)(2,1)} %mw_hbm.1, f32[4,512]{1,0:T(4,128)} %g_hbm.1, bf16[512,1536]{1,0:T(8,128)(2,1)} %ai_hbm.1, ...), custom_call_target="tpu_custom_call" | custom-call | flops 40000000000 | bytes 16000000 | tf_op jit(solution)/shard_map/whole/pallas_call | solution.py:532
  101.8 1.4 %flush.1 = bf16[128,64,128]{2,1,0:T(8,128)(2,1)} custom-call(bf16[128,64,128]{2,1,0:T(8,128)(2,1)S(1)} %whole.1.made_ref), custom_call_target="tpu_custom_call" | custom-call | flops 1000000 | bytes 4000000 | tf_op jit(solution)/shard_map/flush/pallas_call | solution.py:544

commit v5 on v4

--- a/solution.py
+++ b/solution.py
@@ -149,7 +149,7 @@
     pieces += [(x_hbm.at[at], xv.at[at]) for at in rests]
     pieces += [(g_hbm, g_ref), (ai_hbm, ai_ref), (ao_hbm, ao_ref), (di_hbm, di_ref), (do_hbm, do_ref), (ew_hbm, ew_ref)]
     loads = [pltpu.make_async_copy(a, b, load_sem.at[i]) for i, (a, b) in enumerate(pieces)]
-    for load in loads:
+    for load in loads[: bands + 3]:
         load.start()
 
     barrier = pltpu.get_barrier_semaphore()
@@ -159,6 +159,8 @@
         return carry
 
     lax.fori_loop(1, count, greet, 0)
+    for load in loads[bands + 3 :]:
+        load.start()
 
     def widen(r, carry):
         for k in range(4):
@@ -180,9 +182,6 @@
             xs[pl.ds((at + 2) * pitch + LEAD, breadth), :] = xv[at].astype(F32)
     loads[bands].wait()
     pair_kernel(k1_ref, w1_ref)
-    loads[bands + 1].wait()
-    pair_kernel(k2_ref, w2_ref)
-    loads[bands + 2].wait()
 
     def fill(start, n):
         for r in range(n):
@@ -277,6 +276,10 @@
         for start in base:
             fill(start + 4 - 2 * more, 2 * units + 2 * more)
         conv_one([start + 2 - more for start in base], 2 * units + more)
+        if fresh:
+            loads[bands + 1].wait()
+            pair_kernel(k2_ref, w2_ref)
+            loads[bands + 2].wait()
         tail(base, (steps + j) * block + low * span, units)
 
     def early_post(j, low, units):

time: 103 us -> 103 us (level)
  no operation moved by 1% of the time
where the time goes in v5:
time: 103 us
  Pallas kernels  103 us (100%)
    pallas_call x1, Pallas kernels, per_device(): pl.pallas_call(functools.partial(whole_body, geo), in_specs=[pl.BlockSpec...  102 us

profile of v5, /device:TPU:0, one launch (start us, length us, event | category | flops | bytes accessed | tf_op | source)
XLA Modules:
  0.0 103.0 jit_solution(7429734165897682804)
XLA Ops:
  0.0 101.6 %whole.1.made_ref = bf16[128,64,128]{2,1,0:T(8,128)(2,1)S(1)} custom-call(bf16[128,64,128]{2,1,0:T(8,128)(2,1)} %x_hbm.1, bf16[3,3,128,128]{3,2,1,0:T(8,128)(2,1)} %k1_hbm.1, bf16[3,3,128,128]{3,2,1,0:T(8,128)(2,1)} %k2_hbm.1, bf16[512,512]{1,0:T(8,128)(2,1)} %mw_hbm.1, f32[4,512]{1,0:T(4,128)} %g_hbm.1, bf16[512,1536]{1,0:T(8,128)(2,1)} %ai_hbm.1, ...), custom_call_target="tpu_custom_call" | custom-call | flops 40000000000 | bytes 16000000 | tf_op jit(solution)/shard_map/whole/pallas_call | solution.py:535
  101.6 1.4 %flush.1 = bf16[128,64,128]{2,1,0:T(8,128)(2,1)} custom-call(bf16[128,64,128]{2,1,0:T(8,128)(2,1)S(1)} %whole.1.made_ref), custom_call_target="tpu_custom_call" | custom-call | flops 1000000 | bytes 4000000 | tf_op jit(solution)/shard_map/flush/pallas_call | solution.py:547
